TPU v7x, 256 devices: a whole 4x4x8 slice. The times are simulated.
256 devices in a mesh: gx: 16 (over z, x_lo), gy: 16 (over y, x_hi, core).
Axes of the slice: x: 4 (x_hi: 2, x_lo: 2; x = x_hi * 2 + x_lo), y: 4, z: 8, core: 2. Of those that a mesh axis runs over, the one named last changes fastest.
Arguments:
- pooled: bfloat16 [32768, 8, 128], P(('gx', 'gy')), may hold values from -6 to 6
- cotangent: bfloat16 [32768, 28, 128], P(('gx', 'gy')), may hold values from -0.03125 to 0.03125
- bilinear: bfloat16 [7, 128, 128], replicated, may hold values from -0.5 to 0.5
- bag_ids: int32 [32768, 8, 4], P(('gx', 'gy')), may hold values from 0 to 65535, as said below
- bag_lens: int32 [32768, 8], P(('gx', 'gy')), may hold values from 1 to 4
- row_home: int32 [8, 65536], replicated, may hold values from 0 to 65535, as said below
Outputs:
- weight_grad: float32 [7, 128, 128], replicated
- table_grad: float32 [65536, 8, 128], P(('gx', 'gy'))
Inputs may be any that keep to these rules, and one draw needn't show every extreme that they name: Each row row_home[f] is a permutation; row r of field f's table is stored at position row_home[f, r] of table_grad's first dimension. Only the first bag_lens entries of a bag are live. The stored position q = row_home[f, bag_ids[sample, f, k]] of an entry lies in the block of 256 positions of device q // 256 (devices in gx+gy order); among all entries of one device's samples, live or not, at most 32 lie in any one device's block; in every device's entries some block is hit exactly 32 times, and one block is hit exactly 32 times by the entries of every device.
All inputs are finite; a program needn't handle non-finite values.
Results may differ from a plain program's by a relative error of at most 0.0035.
Values may be sent and summed in bfloat16 or wider, within the bound.
A program may use at most 64 MiB of HBM per device.

v0:
```python
import jax
import jax.numpy as jnp
from jax import lax
from jax.sharding import PartitionSpec as P

FIELDS = 8
BAG = 4
R_DEV = 256


def cut_along(x, dim, length):
    shape = x.shape
    blocks = x.reshape(*shape[:dim], length, shape[dim] // length, *shape[dim + 1 :])
    return jnp.moveaxis(blocks, dim, 0)


def joined_along(blocks, dim):
    shape = list(blocks.shape[1:])
    shape[dim] *= blocks.shape[0]
    return jnp.moveaxis(blocks, 0, dim).reshape(shape)


def exchange_both(x, axis, axes, splits, concats):
    sizes = [lax.axis_size(a) for a in axes]
    blocks = cut_along(x, splits[0], sizes[0])
    blocks = jnp.moveaxis(cut_along(blocks, splits[1] + 1, sizes[1]), 0, 1)
    inside = blocks.shape[2:]
    blocks = blocks.reshape(-1, *inside)
    blocks = lax.all_to_all(blocks, axis, split_axis=0, concat_axis=0, tiled=True)
    blocks = joined_along(blocks.reshape(*sizes, *inside), concats[0] + 1)
    return joined_along(blocks, concats[1])


def pair_list(fields):
    return [(i, j) for i in range(fields) for j in range(i + 1, fields)]


def on_device(pooled, cotangent, bilinear, bag_ids, bag_lens, row_home):
    pair_order = pair_list(FIELDS)
    samples = pooled.shape[0]
    width = pooled.shape[2]
    projected = jnp.einsum(
        "bfd,fde->bfe", pooled[:, : FIELDS - 1], bilinear, preferred_element_type=jnp.float32
    )
    upper_terms = []
    for i in range(FIELDS - 1):
        running = jnp.zeros((samples, width), jnp.float32)
        for p, (a, c) in enumerate(pair_order):
            if a == i:
                running = running + cotangent[:, p].astype(jnp.float32) * pooled[:, c].astype(
                    jnp.float32
                )
        upper_terms.append(running)
    upper_bf = jnp.stack(upper_terms, 1).astype(jnp.bfloat16)
    local_weight = jnp.einsum(
        "bfd,bfe->fde", pooled[:, : FIELDS - 1], upper_bf, preferred_element_type=jnp.float32
    )
    weight_grad = lax.psum(local_weight, ("gx", "gy"))
    back_terms = jnp.einsum("bfe,fde->bfd", upper_bf, bilinear, preferred_element_type=jnp.float32)
    field_list = []
    for i in range(FIELDS):
        running = back_terms[:, i] if i < FIELDS - 1 else jnp.zeros((samples, width), jnp.float32)
        for p, (a, c) in enumerate(pair_order):
            if c == i:
                running = running + cotangent[:, p].astype(jnp.float32) * projected[:, a]
        field_list.append(running)
    field_grads = jnp.stack(field_list, 1).astype(jnp.bfloat16)
    size_gx = lax.axis_size("gx")
    size_gy = lax.axis_size("gy")
    owners_all = size_gx * size_gy
    entries = samples * FIELDS * BAG
    capacity = max(1, 2 * entries // owners_all)
    sentinel = R_DEV * FIELDS
    field_index = jnp.arange(FIELDS, dtype=jnp.int32)[None, :, None]
    stored = row_home[field_index, bag_ids]
    live = jnp.arange(BAG, dtype=jnp.int32)[None, None, :] < bag_lens[:, :, None]
    owner = (stored // R_DEV).reshape(-1)
    target = jnp.where(live, stored % R_DEV * FIELDS + field_index, sentinel).reshape(-1)
    values = jnp.where(live[:, :, :, None], field_grads[:, :, None, :], jnp.zeros((), jnp.bfloat16))
    values = values.reshape(entries, width)
    block_rows = 128
    blocks = entries // block_rows
    owner_ids = jnp.arange(owners_all, dtype=jnp.int32)
    owner_table = (owner.reshape(blocks, block_rows, 1) == owner_ids[None, None, :]).astype(
        jnp.bfloat16
    )
    row_pos = jnp.arange(block_rows, dtype=jnp.int32)
    earlier = (row_pos[:, None] > row_pos[None, :]).astype(jnp.bfloat16)
    within_all = jnp.einsum("ij,bjo->bio", earlier, owner_table, preferred_element_type=jnp.float32)
    block_totals = jnp.sum(owner_table.astype(jnp.float32), axis=1)
    block_start = jnp.cumsum(block_totals, axis=0) - block_totals
    ahead = within_all + block_start[:, None, :]
    rank = jnp.sum(ahead * owner_table.astype(jnp.float32), axis=2).reshape(-1).astype(jnp.int32)
    place = owner * capacity + rank
    send_values = (
        jnp.zeros((owners_all * capacity, width), jnp.bfloat16)
        .at[place]
        .set(values, unique_indices=True)
    )
    send_target = (
        jnp.full((owners_all * capacity,), sentinel, jnp.int32)
        .at[place]
        .set(target, unique_indices=True)
    )
    send_values = send_values.reshape(size_gx, size_gy, capacity, width)
    send_target = send_target.reshape(size_gx, size_gy, capacity)
    got_values, got_target = (
        exchange_both(send_values, ("gx", "gy"), ("gx", "gy"), (0, 1), (0, 1)),
        exchange_both(send_target, ("gx", "gy"), ("gx", "gy"), (0, 1), (0, 1)),
    )
    summed = jax.ops.segment_sum(
        got_values.reshape(-1, width).astype(jnp.float32),
        got_target.reshape(-1),
        num_segments=sentinel + 1,
    )
    table_grad = summed[:sentinel].reshape(R_DEV, FIELDS, width)
    return (weight_grad, table_grad)


def solution(mesh):
    placed = (
        P(("gx", "gy"), None, None),
        P(("gx", "gy"), None, None),
        P(),
        P(("gx", "gy"), None, None),
        P(("gx", "gy"), None),
        P(),
    )
    return jax.shard_map(
        on_device,
        mesh=mesh,
        in_specs=placed,
        out_specs=(P(), P(("gx", "gy"), None, None)),
        check_vma=False,
    )
```

profile of v0, /device:TPU:1, one launch (start us, length us, event | category | flops | bytes accessed | tf_op | source)
XLA Modules:
  0.0 465.0 jit_solution(641555392730720194)
XLA Ops:
  7.2 0.9 fusion.101
  8.8 25.5 %gather_fusion = s32[4096]{0:T(1024)S(1)} fusion(s32[8,65536]{1,0:T(8,128)S(1)} %copy-done, s32[4096]{0:T(1024)S(1)} %reshape.238), kind=kCustom, calls=%fused_computation | custom fusion | bytes 65536 | tf_op jit(solution)/shard_map/gather | solution.py:75
  34.3 0.7 convert_reduce_fusion
  35.1 1.7 fusion
  37.9 15.5 %scatter_custom_fusion = s32[8192]{0:T(1024)S(1)} fusion(s32[4096]{0:T(1024)S(1)} %bitcast.78, s32[4096]{0:T(1024)S(1)} %fusion.97, s32[]{:T(128)} %constant.25.clone.1), kind=kCustom, calls=%fused_computation.187 | custom fusion | bytes 32772 | tf_op jit(solution)/shard_map/scatter | solution.py:103
  53.4 0.7 reshape_transpose_transpose_reshape_reshape_reshape.6
  54.2 15.6 %all-to-all-start = ((s32[256,1,1,32]{3,2,1,0:T(1,128)}), s32[256,1,1,32]{3,2,1,0:T(1,128)S(1)}, u32[]{:S(2)}, u32[]{:S(2)}) async-start(s32[256,1,1,32]{3,2,1,0:T(1,128)} %bitcast.8), calls=%async_computation | async-start | bytes 262144 | tf_op jit(solution)/shard_map/all_to_all | solution.py:29
  69.8 1.5 fusion.107
  71.3 1.8 fusion.106
  74.1 0.7 copy.140
  74.8 0.9 copy.142
  75.7 0.9 copy.144
  76.6 0.7 copy.146
  77.3 0.9 copy.148
  78.2 0.7 copy.150
  78.9 0.9 copy.152
  79.9 0.7 copy.143
  80.7 0.7 copy.141
  81.4 0.7 copy.156
  82.2 0.7 copy.158
  83.3 0.9 copy.160
  84.2 1.5 copy.161
  85.7 0.9 copy.162
  86.5 0.7 copy.163
  87.3 0.9 copy.164
  88.1 0.7 copy.165
  88.9 0.9 copy.166
  89.7 0.9 copy.167
  90.7 0.9 copy.169
  91.6 0.9 copy.170
  92.5 0.9 copy.171
  93.4 0.9 copy.172
  94.4 0.9 copy.174
  95.3 0.9 fusion.92
  96.2 0.9 fusion.84
  97.1 0.8 fusion.83
  97.9 0.8 fusion.82
  99.6 0.8 fusion.90
  100.4 0.8 fusion.89
  101.5 0.9 copy.135
  102.4 1.3 broadcast_in_dim.61
  103.7 14.8 %scatter_custom_fusion.1 = bf16[8192,128]{1,0:T(8,128)(2,1)} fusion(s32[4096]{0:T(1024)} %bitcast.79, bf16[4096,128]{1,0:T(8,128)(2,1)S(1)} %bitcast.73, bf16[]{:T(256)} %constant.51.clone.1, pred[4096]{0:T(1024)(128)(4,1)S(1)} %lt.51), kind=kCustom, calls=%fused_computation.17 | custom fusion | flops 524288 | bytes 3150848 | tf_op jit(solution)/shard_map/scatter | solution.py:98
  118.5 14.7 %all-to-all-start.1 = ((bf16[256,1,1,32,128]{4,3,2,1,0:T(8,128)(2,1)}), bf16[256,1,1,32,128]{4,3,2,1,0:T(8,128)(2,1)}, u32[]{:S(2)}, u32[]{:S(2)}) async-start(bf16[256,1,1,32,128]{4,3,2,1,0:T(8,128)(2,1)} %bitcast.72), calls=%async_computation.1 | async-start | bytes 4194304 | tf_op jit(solution)/shard_map/all_to_all | solution.py:29
  133.3 1.0 convolution_bitcast_fusion.2
  134.4 264.4 %all-reduce.2.cloned.1.call-done = f32[7,128,128]{1,2,0:T(8,128)} async-done(((f32[7,128,128]{1,2,0:T(8,128)}), f32[7,128,128]{1,2,0:T(8,128)}) %all-reduce.2.cloned.1.call-update) | async-done | bytes 458768 | tf_op jit(solution)/shard_map/psum | solution.py:58
  398.8 2.0 copy.136
  400.8 56.3 %scatter_custom_fusion.2 = f32[2049,128]{1,0:T(8,128)S(1)} fusion(s32[8192]{0:T(1024)S(1)} %reshape.262, bf16[8192,128]{1,0:T(8,128)(2,1)} %bitcast.31, f32[]{:T(128)} %constant.21.clone.1), kind=kCustom, calls=%fused_computation.7 | custom fusion | flops 2097152 | bytes 3146244 | tf_op jit(solution)/shard_map/scatter-add | solution.py:111
  457.2 1.0 slice_bitcast_fusion
  (87 shorter events, 4.7 us)
Async XLA Ops:
  7.2 1.6 copy-start
  35.0 1.7 copy-start.22
  36.7 36.4 %copy-start.1 = (bf16[128,8,128]{2,1,0:T(8,128)(2,1)S(1)}, bf16[128,8,128]{2,1,0:T(8,128)(2,1)}, u32[]{:S(2)}) copy-start(bf16[128,8,128]{2,1,0:T(8,128)(2,1)} %param.6) | copy-start | bytes 786436
  37.8 16.3 %copy-start.21 = (s32[4096,1]{0,1:T(1,128)}, s32[4096,1]{0,1:T(1,128)S(1)}, u32[]{:S(2)}) copy-start(s32[4096,1]{0,1:T(1,128)S(1)} %compare_select_fusion) | copy-start | bytes 49156
  54.2 64.4 %all-to-all-start = ((s32[256,1,1,32]{3,2,1,0:T(1,128)}), s32[256,1,1,32]{3,2,1,0:T(1,128)S(1)}, u32[]{:S(2)}, u32[]{:S(2)}) async-start(s32[256,1,1,32]{3,2,1,0:T(1,128)} %bitcast.8), calls=%async_computation | async-start | bytes 262144 | tf_op jit(solution)/shard_map/all_to_all | solution.py:29
  74.8 24.1 %copy-start.4 = (bf16[7,128,128]{2,1,0:T(8,128)(2,1)S(1)}, bf16[7,128,128]{2,1,0:T(8,128)(2,1)}, u32[]{:S(2)}) copy-start(bf16[7,128,128]{2,1,0:T(8,128)(2,1)} %param.8) | copy-start | bytes 688132
  75.7 23.2 %copy-start.6 = (bf16[128,1,128]{0,2,1:T(8,128)(2,1)}, bf16[128,1,128]{0,2,1:T(8,128)(2,1)S(1)}, u32[]{:S(2)}) copy-start(bf16[128,1,128]{0,2,1:T(8,128)(2,1)S(1)} %copy.142) | copy-start | bytes 98308
  76.6 22.3 %copy-start.5 = (bf16[128,1,128]{0,2,1:T(8,128)(2,1)}, bf16[128,1,128]{0,2,1:T(8,128)(2,1)S(1)}, u32[]{:S(2)}) copy-start(bf16[128,1,128]{0,2,1:T(8,128)(2,1)S(1)} %copy.144) | copy-start | bytes 98308
  90.6 8.3 %copy-start.7 = (bf16[128,1,128]{0,2,1:T(8,128)(2,1)}, bf16[128,1,128]{0,2,1:T(8,128)(2,1)S(1)}, u32[]{:S(2)}) copy-start(bf16[128,1,128]{0,2,1:T(8,128)(2,1)S(1)} %copy.167) | copy-start | bytes 98308
  92.5 6.4 %copy-start.9 = (bf16[128,1,128]{0,2,1:T(8,128)(2,1)}, bf16[128,1,128]{0,2,1:T(8,128)(2,1)S(1)}, u32[]{:S(2)}) copy-start(bf16[128,1,128]{0,2,1:T(8,128)(2,1)S(1)} %copy.170) | copy-start | bytes 98308
  94.3 4.7 %copy-start.11 = (bf16[128,1,128]{0,2,1:T(8,128)(2,1)}, bf16[128,1,128]{0,2,1:T(8,128)(2,1)S(1)}, u32[]{:S(2)}) copy-start(bf16[128,1,128]{0,2,1:T(8,128)(2,1)S(1)} %copy.172) | copy-start | bytes 98308
  95.3 4.3 copy-start.14
  96.2 5.0 %copy-start.13 = (bf16[128,1,128]{0,2,1:T(8,128)(2,1)S(1)}, bf16[128,1,128]{0,2,1:T(8,128)(2,1)}, u32[]{:S(2)}) copy-start(bf16[128,1,128]{0,2,1:T(8,128)(2,1)} %copy.165) | copy-start | bytes 98308
  96.2 5.0 %copy-start.16 = (bf16[128,1,128]{0,2,1:T(8,128)(2,1)S(1)}, bf16[128,1,128]{0,2,1:T(8,128)(2,1)}, u32[]{:S(2)}) copy-start(bf16[128,1,128]{0,2,1:T(8,128)(2,1)} %copy.156) | copy-start | bytes 98308
  96.2 5.0 %copy-start.18 = (bf16[128,1,128]{0,2,1:T(8,128)(2,1)S(1)}, bf16[128,1,128]{0,2,1:T(8,128)(2,1)}, u32[]{:S(2)}) copy-start(bf16[128,1,128]{0,2,1:T(8,128)(2,1)} %copy.161) | copy-start | bytes 98308
  96.2 5.0 %copy-start.20 = (bf16[128,1,128]{0,2,1:T(8,128)(2,1)S(1)}, bf16[128,1,128]{0,2,1:T(8,128)(2,1)}, u32[]{:S(2)}) copy-start(bf16[128,1,128]{0,2,1:T(8,128)(2,1)} %copy.146) | copy-start | bytes 98308
  98.8 2.5 copy-start.15
  98.8 2.5 copy-start.17
  98.8 2.5 copy-start.19
  98.9 2.5 copy-start.2
  99.2 2.2 copy-start.8
  99.2 2.2 copy-start.10
  99.2 2.2 copy-start.12
  118.5 14.8 %copy-start.3 = (bf16[128,7,128]{0,2,1:T(8,128)(2,1)S(1)}, bf16[128,7,128]{0,2,1:T(8,128)(2,1)}, u32[]{:S(2)}) copy-start(bf16[128,7,128]{0,2,1:T(8,128)(2,1)} %copy-done.2) | copy-start | bytes 688132
  118.5 282.3 %all-to-all-start.1 = ((bf16[256,1,1,32,128]{4,3,2,1,0:T(8,128)(2,1)}), bf16[256,1,1,32,128]{4,3,2,1,0:T(8,128)(2,1)}, u32[]{:S(2)}, u32[]{:S(2)}) async-start(bf16[256,1,1,32,128]{4,3,2,1,0:T(8,128)(2,1)} %bitcast.72), calls=%async_computation.1 | async-start | bytes 4194304 | tf_op jit(solution)/shard_map/all_to_all | solution.py:29
  133.2 265.6 %all-reduce.2.cloned.1.call-start = ((), (), s32[]{:S(2)}) async-start(), calls=%async_computation.2 | async-start | bytes 917504 | tf_op jit(solution)/shard_map/psum | solution.py:58
Sparse Core Ops, SparseCore 0:
  140.1 258.6 all-reduce.1
where the time goes:
time: 467 us; the launch traced here: 465 us
  waiting for transfers between devices  264 us (57%)
  other arithmetic  78.5 us (17%)
  local copies, waits for them, and re-layouts  73.9 us (16%)
  starting transfers between devices  30.4 us (7%)
  between operations  14.6 us (3%)
    psum x1, waiting for transfers between devices, on_device(): weight_grad = lax.psum(local_weight, ('gx', 'gy'))  264 us
    scatter-add x1, other arithmetic, on_device(): jax.ops.segment_sum(got_values.reshape(-1, width).astype(jnp.float32), go...  56.3 us
    all_to_all x2, starting transfers between devices, exchange_both(): lax.all_to_all(blocks, axis, split_axis=0, concat_axis=0, tiled=True)  30.4 us
    gather x1, local copies, waits for them, and re-layouts, on_device(): stored = row_home[field_index, bag_ids]  25.5 us
    unnamed x84, local copies, waits for them, and re-layouts  23.9 us
    scatter x1, local copies, waits for them, and re-layouts, on_device(): send_target = jnp.full((owners_all * capacity,), sentinel, jnp.int32).at[...  15.5 us
    scatter x1, other arithmetic, on_device(): send_values = jnp.zeros((owners_all * capacity, width), jnp.bfloat16).at[...  14.8 us
  transfers between devices with their start and end apart: 3, of which 1 were waited for; matrix products, arithmetic and copies ran while one was open for 11% of the time, Pallas kernels for 0%

commit v1 on v0

v1 whole, which is shorter than its diff:
```python
import functools

import jax
import jax.numpy as jnp
from jax import lax
from jax.experimental import pallas as pl
from jax.experimental.pallas import tpu as pltpu
from jax.sharding import PartitionSpec as P

MESH = pl.DeviceIdType.MESH
F = 8
BAG = 4
D = 128
TOK = 128
CAP = 32
NZ = 8
NP = 32
ROWS = F * TOK
NCH = 2
RED = 28
PAIR = {(i, j): p for p, (i, j) in enumerate((i, j) for i in range(F) for j in range(i + 1, F))}
F32, BF16, I32 = jnp.float32, jnp.bfloat16, jnp.int32


def dev(z, p):
    return (2 * z + p // 16, p % 16)


def iota(shape, dim):
    return lax.broadcasted_iota(I32, shape, dim)


def onehot(mask):
    return jnp.where(mask, 1.0, 0.0).astype(BF16)


def dot(a, b, ca=1, cb=0):
    return lax.dot_general(a, b, (((ca,), (cb,)), ((), ())), preferred_element_type=F32)


def body(
    pool_h, cot_h, bil_h, ids_h, lens_h, home_h,
    wg_o, acc_o,
    pool, cot, bil, ids, lens, home,
    pf, up, proj, back, share,
    own, loc, live, m4, mall, dsend, drecv, cbuf,
    vbuf, stage, got, amat, bmat,
    w2, w3, w4, part,
    lsem, zs, zr, ms, mr, ds_, dr, ss, rr, ws, wr,
):
    gx, gy = lax.axis_index("gx"), lax.axis_index("gy")
    z, me = gx // 2, (gx % 2) * 16 + gy
    up_z, dn_z = (z + 1) % NZ, (z + 7) % NZ

    loads = [
        pltpu.make_async_copy(a, b, lsem.at[n])
        for n, (a, b) in enumerate(
            [(pool_h, pool), (bil_h, bil), (cot_h, cot), (ids_h, ids), (lens_h, lens), (home_h, home)]
        )
    ]
    for c in loads:
        c.start()

    bar = pltpu.get_barrier_semaphore()

    @pl.loop(1, NP)
    def _(j):
        pl.semaphore_signal(bar, inc=1, device_id=dev(z, me ^ j), device_id_type=MESH)

    @pl.loop(1, NZ)
    def _(t):
        pl.semaphore_signal(bar, inc=1, device_id=dev((z + t) % NZ, me), device_id_type=MESH)

    loads[0].wait()
    perm = onehot(iota((128, 128), 1) == (iota((128, 128), 0) % 16) * F + iota((128, 128), 0) // 16)
    x = jnp.concatenate([pool[pl.ds(g * 128, 128), :] for g in range(8)], axis=1)
    y = dot(perm, x).astype(BF16)
    for g in range(8):
        for f in range(F):
            pf[f, pl.ds(g * 16, 16), :] = y[f * 16 : f * 16 + 16, g * 128 : g * 128 + 128]
    loads[1].wait()
    for i in range(F - 1):
        proj[i] = dot(pf[i], bil[i])
    loads[2].wait()

    @pl.loop(0, 8)
    def _(r):
        rows = pl.ds(pl.multiple_of(r * 16, 16), 16)
        pj = [pf[j, rows, :].astype(F32) for j in range(F)]
        for i in range(F - 1):
            run = cot[PAIR[i, i + 1], rows, :].astype(F32) * pj[i + 1]
            for j in range(i + 2, F):
                run = run + cot[PAIR[i, j], rows, :].astype(F32) * pj[j]
            up[i, rows, :] = run.astype(BF16)

    for i in range(F - 1):
        back[i] = dot(up[i], bil[i], 1, 1)
    for i in range(F - 1):
        share[pl.ds(i * 128, 128), :] = dot(pf[i], up[i], 0, 0).astype(BF16)

    @pl.loop(0, 8)
    def _(r):
        rows = pl.ds(pl.multiple_of(r * 16, 16), 16)
        for i in range(F):
            run = back[i, rows, :] if i < F - 1 else cot[PAIR[0, i], rows, :].astype(F32) * proj[0, rows, :]
            for k in range(0 if i < F - 1 else 1, i):
                run = run + cot[PAIR[k, i], rows, :].astype(F32) * proj[k, rows, :]
            vbuf[0, pl.ds(pl.multiple_of(i * 128 + r * 16, 16), 16), :] = run.astype(BF16)

    pl.semaphore_wait(bar, NP - 1 + NZ - 1)

    half = ROWS // NCH

    def zcopy(d, t, c):
        src, dst = (t - 1, t) if d == 0 else ((8 - (t - 1)) % 8, 8 - t)
        rows = pl.ds(c * half, half)
        return pltpu.make_async_remote_copy(
            vbuf.at[src, rows], vbuf.at[dst, rows], zs.at[d, t - 1, c], zr.at[d, t - 1, c],
            device_id=dev(up_z if d == 0 else dn_z, me), device_id_type=MESH,
        )

    def zcopy_wait(d, t, c):
        zcopy(d, t, c).wait_recv()

    for c in range(NCH):
        for d in range(2):
            zcopy(d, 1, c).start()

    def w2copy(r):
        return pltpu.make_async_remote_copy(
            share.at[pl.ds(pl.multiple_of(r * 32, 32), 32)], w2.at[me], ws.at[0], wr.at[0],
            device_id=dev(z, r), device_id_type=MESH,
        )

    @pl.loop(0, NP)
    def _(j):
        r = me ^ j

        @pl.when((r < RED) & (j > 0))
        def _():
            w2copy(r).start()

    loads[3].wait()
    loads[4].wait()
    loads[5].wait()
    hi_iota, lo_iota = iota((512, 128), 0), iota((128, 128), 0)
    for f in range(F):
        t = home[:, f, :]
        table = jnp.concatenate([(t >> 8).astype(F32), (t & 255).astype(F32)], axis=1).astype(BF16)
        idr = ids[f]
        hi, lo = idr >> 7, idr & 127
        oh = jnp.concatenate([onehot(hi_iota == hi[k : k + 1]) for k in range(BAG)], axis=1)
        out = dot(table, oh, 0, 0)
        for k in range(BAG):
            mask = lo_iota == lo[k : k + 1]
            cols = slice(k * 128, k * 128 + 128)
            row = f * BAG + k
            own[row : row + 1, :] = jnp.sum(jnp.where(mask, out[:128, cols], 0.0), axis=0, keepdims=True).astype(I32)
            loc[row : row + 1, :] = jnp.sum(jnp.where(mask, out[128:, cols], 0.0), axis=0, keepdims=True)
            live[row : row + 1, :] = jnp.where(lens[f : f + 1, :] > k, float(f + 1), 0.0)

    upper_tri = jnp.concatenate(
        [onehot(iota((256, 256), 0) < iota((256, 256), 1)), jnp.ones((256, 128), BF16)], axis=1
    )
    own_iota = iota((256, 256), 0)
    o4_iota, rr_iota = iota((64, 256), 0), iota((128, 256), 0)
    lane = (iota((1, 256), 1) % 128).astype(F32)

    def rank_block(j, carry):
        before, table = carry
        two = lambda ref: jnp.concatenate([ref[pl.ds(2 * j, 1), :], ref[pl.ds(2 * j + 1, 1), :]], axis=1)
        o = two(own)
        hit = own_iota == o
        res = dot(onehot(hit), upper_tri)
        ahead = res[:, :256] + jnp.concatenate([before, before], axis=1)
        rank = jnp.sum(jnp.where(hit, ahead, 0.0), axis=0, keepdims=True).astype(I32)
        spot = rr_iota == (o & 3) * CAP + rank
        pay = [jnp.where(spot, v, 0.0).astype(BF16) for v in (lane, two(live), two(loc))]
        table = table + dot(onehot(o4_iota == (o >> 2)), jnp.concatenate(pay, axis=0), 1, 1)
        return before + res[:, 256:], table

    _, table = lax.fori_loop(0, 16, rank_block, (jnp.zeros((256, 128), F32), jnp.zeros((64, 384), F32)))
    m4[...] = (table[:, :128] + 128.0 * table[:, 128:256] + 2048.0 * table[:, 256:]).astype(I32)
    mall[0] = m4[pl.ds(pl.multiple_of(z * 8, 8), 8), :]

    def mcopy(t):
        to = (z + t) % NZ
        return pltpu.make_async_remote_copy(
            m4.at[pl.ds(pl.multiple_of(to * 8, 8), 8)], mall.at[t], ms, mr, device_id=dev(to, me), device_id_type=MESH
        )

    @pl.loop(1, NZ)
    def _(t):
        mcopy(t).start()

    lane128 = iota((128, 128), 1)

    def gather(idx):
        for pq in range(8):
            row = mall[idx, pl.ds(pq, 1), :] & 2047
            col = jnp.broadcast_to(row, (128, 128)).T
            g = jnp.concatenate([onehot(col == lane128 + 128 * (f + 1)) for f in range(F)], axis=1)
            rows = dot(g, vbuf[idx]).astype(BF16)
            stage[idx, pl.ds(pq * 4, 4)] = rows.reshape(4, CAP, D)

    def xycopy(idx, q):
        return pltpu.make_async_remote_copy(
            stage.at[idx, q], got.at[idx, me], ss.at[idx], rr.at[idx], device_id=dev(z, q), device_id_type=MESH
        )

    def send(idx):
        got[idx, me] = stage[idx, me]

        @pl.loop(1, NP)
        def _(j):
            xycopy(idx, me ^ j).start()

    q_iota = iota((256, 128), 0)

    def accumulate(idx):
        peers = got.at[idx, pl.ds(0, NP - 1)]
        pltpu.make_async_copy(peers, peers, rr.at[idx]).wait()
        code = cbuf[idx]
        fcode = (code >> 7) & 15
        lcode = code >> 11
        for g in range(8):
            fcol = jnp.broadcast_to(fcode[g : g + 1, :].astype(F32), (128, 128)).T.astype(BF16)
            v = got[idx, pl.ds(g * 4, 4)].reshape(128, D)
            rows = pl.ds(g * 128, 128)
            for f in range(F):
                bmat[rows, f * D : f * D + D] = jnp.where(fcol == jnp.asarray(f + 1, BF16), v, jnp.zeros_like(v))
            amat[:, g * 128 : g * 128 + 128] = onehot(q_iota == lcode[g : g + 1, :])
        acc_o[...] += dot(amat[...], bmat[...])

    def dcopy(q):
        return pltpu.make_async_remote_copy(
            dsend.at[q], drecv.at[me], ds_, dr, device_id=dev(z, q), device_id_type=MESH
        )

    def targets_out():
        many = mall.at[pl.ds(1, NZ - 1)]
        pltpu.make_async_copy(many, many, mr).wait()
        mine = iota((8, 128), 1) // CAP == me % 4
        for pq in range(8):
            x = mall[:, pq, :]
            for s in range(4):
                y = pltpu.roll(x, s * CAP, 1) if s else x
                dsend[pq * 4 + (me % 4 + 4 - s) % 4] = jnp.where(mine, y, 0)
        drecv[me] = dsend[me]

        @pl.loop(1, NP)
        def _(j):
            dcopy(me ^ j).start()

    def targets_in():
        many = drecv.at[pl.ds(0, NP - 1)]
        pltpu.make_async_copy(many, many, dr).wait()
        for g in range(8):
            cbuf[:, g, :] = drecv[4 * g] + drecv[4 * g + 1] + drecv[4 * g + 2] + drecv[4 * g + 3]

    def w3copy(t):
        return pltpu.make_async_remote_copy(
            part, w3.at[z], ws.at[1], wr.at[1], device_id=dev((z + t) % NZ, me), device_id_type=MESH
        )

    def w4copy(q):
        return pltpu.make_async_remote_copy(
            w4.at[me], w4.at[me], ws.at[2], wr.at[2], device_id=dev(z, q), device_id_type=MESH
        )

    def weight_add():
        @pl.when(me < RED)
        def _():
            peers = w2.at[pl.ds(0, NP - 1)]
            w2[me] = share[pl.ds(pl.multiple_of(me * 32, 32), 32), :]
            pltpu.make_async_copy(peers, peers, wr.at[0]).wait()
            total = w2[0].astype(F32)
            for i in range(1, NP):
                total = total + w2[i].astype(F32)
            part[...] = total
            w3[z] = total

            @pl.loop(1, NZ)
            def _(t):
                w3copy(t).start()

    def weight_spread():
        @pl.when(me < RED)
        def _():
            peers = w3.at[pl.ds(0, NZ - 1)]
            pltpu.make_async_copy(peers, peers, wr.at[1]).wait()
            total = w3[0]
            for i in range(1, NZ):
                total = total + w3[i]
            w4[me] = total.astype(BF16)

            @pl.loop(1, NP)
            def _(j):
                w4copy(me ^ j).start()

    def at(n):
        return jnp.where(n == 7, 4, jnp.where(n % 2 == 1, (n + 1) // 2, (8 - n // 2) % 8))

    acc_o[...] = jnp.zeros_like(acc_o)

    @pl.loop(0, 9)
    def _(n):
        t = (n + 1) // 2

        @pl.when((n % 2 == 1) & (n < 7))
        def _():
            for c in range(NCH):
                for d in range(2):
                    zcopy_wait(d, t, c)

                    @pl.when((t < 3) | ((c < NCH // 2) == (d == 0)))
                    def _():
                        zcopy(d, t + 1, c).start()

        @pl.when(n == 7)
        def _():
            for c in range(NCH // 2):
                zcopy_wait(0, 4, c)
                zcopy_wait(1, 4, c + NCH // 2)

        @pl.when(n == 1)
        def _():
            targets_out()
            weight_add()

        @pl.when(n < 8)
        def _():
            gather(at(n))
            send(at(n))

        @pl.when(n == 2)
        def _():
            targets_in()

        @pl.when(n == 4)
        def _():
            weight_spread()

        @pl.when(n >= 2)
        def _():
            accumulate(at(n - 1))

        @pl.when(n == 2)
        def _():
            accumulate(0)

    @pl.when(me < RED)
    def _():
        peers = w4.at[pl.ds(0, RED - 1)]
        pltpu.make_async_copy(peers, peers, wr.at[2]).wait()

    @pl.when(me >= RED)
    def _():
        pltpu.make_async_copy(w4, w4, wr.at[2]).wait()

    wg_o[...] = w4[...]
    for t in range(1, 5):
        for d in range(2):
            for c in range(NCH):
                if t < 4 or (c < NCH // 2) == (d == 0):
                    zcopy(d, t, c).wait_send()
    many = mall.at[pl.ds(0, NZ - 1)]
    pltpu.make_async_copy(many, many, ms).wait()
    many = dsend.at[pl.ds(0, NP - 1)]
    pltpu.make_async_copy(many, many, ds_).wait()
    for k in range(8):
        many = stage.at[k, pl.ds(0, NP - 1)]
        pltpu.make_async_copy(many, many, ss.at[k]).wait()

    @pl.when(me < RED)
    def _():
        many = w2.at[pl.ds(0, RED - 1)]
        pltpu.make_async_copy(many, many, ws.at[0]).wait()
        many = w3.at[pl.ds(0, NZ - 1)]
        pltpu.make_async_copy(many, many, ws.at[1]).wait()
        many = w2.at[pl.ds(0, NP - 1)]
        pltpu.make_async_copy(many, many, ws.at[2]).wait()

    @pl.when(me >= RED)
    def _():
        many = w2.at[pl.ds(0, RED)]
        pltpu.make_async_copy(many, many, ws.at[0]).wait()


def on_device(pooled, cotangent, bilinear, bag_ids, bag_lens, row_home):
    any_ = pl.BlockSpec(memory_space=pl.ANY)
    vm = pl.BlockSpec(memory_space=pltpu.VMEM)
    dma = pltpu.SemaphoreType.DMA
    wg, acc = pl.pallas_call(
        body,
        out_shape=(
            jax.ShapeDtypeStruct((RED, 32, D), BF16),
            jax.ShapeDtypeStruct((256, F * D), F32),
        ),
        in_specs=[any_] * 6,
        out_specs=(vm, vm),
        scratch_shapes=[
            pltpu.VMEM((ROWS, D), BF16),
            pltpu.VMEM((28, TOK, D), BF16),
            pltpu.VMEM((F - 1, D, D), BF16),
            pltpu.VMEM((F, BAG, TOK), I32),
            pltpu.VMEM((F, TOK), I32),
            pltpu.VMEM((512, F, 128), I32),
            pltpu.VMEM((F, TOK, D), BF16),
            pltpu.VMEM((F - 1, TOK, D), BF16),
            pltpu.VMEM((F - 1, TOK, D), F32),
            pltpu.VMEM((F - 1, TOK, D), F32),
            pltpu.VMEM(((F - 1) * D, D), BF16),
            pltpu.VMEM((F * BAG, 128), I32),
            pltpu.VMEM((F * BAG, 128), F32),
            pltpu.VMEM((F * BAG, 128), F32),
            pltpu.VMEM((64, 128), I32),
            pltpu.VMEM((NZ, 8, 128), I32),
            pltpu.VMEM((NP, 8, 128), I32),
            pltpu.VMEM((NP, 8, 128), I32),
            pltpu.VMEM((NZ, 8, 128), I32),
            pltpu.VMEM((NZ, ROWS, D), BF16),
            pltpu.VMEM((NZ, NP, CAP, D), BF16),
            pltpu.VMEM((NZ, NP, CAP, D), BF16),
            pltpu.VMEM((256, 1024), BF16),
            pltpu.VMEM((1024, F * D), BF16),
            pltpu.VMEM((NP, 32, D), BF16),
            pltpu.VMEM((NZ, 32, D), F32),
            pltpu.VMEM((RED, 32, D), BF16),
            pltpu.VMEM((32, D), F32),
            dma((6,)),
            dma((2, 4, NCH)),
            dma((2, 4, NCH)),
            dma,
            dma,
            dma,
            dma,
            dma((8,)),
            dma((8,)),
            dma((3,)),
            dma((3,)),
        ],
        compiler_params=pltpu.CompilerParams(
            collective_id=0, has_side_effects=True, vmem_limit_bytes=60 * 2**20
        ),
    )(
        pooled.reshape(ROWS, D),
        cotangent.transpose(1, 0, 2),
        bilinear,
        bag_ids.transpose(1, 2, 0),
        bag_lens.transpose(1, 0),
        row_home.reshape(F, 512, 128).transpose(1, 0, 2),
    )
    return wg.reshape(F - 1, D, D).astype(F32), acc.reshape(256, F, D)


def solution(mesh):
    placed = (
        P(("gx", "gy"), None, None),
        P(("gx", "gy"), None, None),
        P(),
        P(("gx", "gy"), None, None),
        P(("gx", "gy"), None),
        P(),
    )
    return jax.shard_map(
        on_device,
        mesh=mesh,
        in_specs=placed,
        out_specs=(P(), P(("gx", "gy"), None, None)),
        check_vma=False,
    )
```

time: 467 us -> 72.1 us (0.15)
  waiting for transfers between devices: 264 us -> 0 us
  other arithmetic: 78.5 us -> 0.8 us
  local copies, waits for them, and re-layouts: 73.9 us -> 2.44 us
  Pallas kernels: 0 us -> 68.1 us
  starting transfers between devices: 30.4 us -> 0 us
  between operations: 14.6 us -> 0.65 us
    psum x1 -> x0, waiting for transfers between devices: 264 us -> none  [on_device(): weight_grad = lax.psum(local_weight, ('gx', 'gy'))]
    pallas_call x0 -> x1, Pallas kernels: none -> 68.1 us  [on_device(): pl.pallas_call(body, out_shape=(jax.ShapeDtypeStruct((RED, 32, D), BF16),...]
    scatter-add x1 -> x0, other arithmetic: 56.3 us -> none  [on_device(): jax.ops.segment_sum(got_values.reshape(-1, width).astype(jnp.float32), go...]
    all_to_all x2 -> x0, starting transfers between devices: 30.4 us -> none  [exchange_both(): lax.all_to_all(blocks, axis, split_axis=0, concat_axis=0, tiled=True)]
    gather x1 -> x0, local copies, waits for them, and re-layouts: 25.5 us -> none  [on_device(): stored = row_home[field_index, bag_ids]]
    unnamed x84 -> x3, local copies, waits for them, and re-layouts: 23.9 us -> 2.44 us
    scatter x1 -> x0, local copies, waits for them, and re-layouts: 15.5 us -> none  [on_device(): send_target = jnp.full((owners_all * capacity,), sentinel, jnp.int32).at[...]
    scatter x1 -> x0, other arithmetic: 14.8 us -> none  [on_device(): send_values = jnp.zeros((owners_all * capacity, width), jnp.bfloat16).at[...]
  transfers between devices with their start and end apart: 3 -> 0, of which waited for: 1 -> 0; matrix products, arithmetic and copies ran while one was open for 11% -> 0% of each run, Pallas kernels for 0% -> 0%
where the time goes in v1:
time: 72.1 us; the launch traced here: 72 us
  Pallas kernels  68.1 us (94%)
  local copies, waits for them, and re-layouts  2.44 us (3%)
  other arithmetic  0.8 us (1%)
    pallas_call x1, Pallas kernels, on_device(): pl.pallas_call(body, out_shape=(jax.ShapeDtypeStruct((RED, 32, D), BF16),...  68.1 us
    unnamed x3, local copies, waits for them, and re-layouts  2.44 us

profile of v1, /device:TPU:1, one launch (start us, length us, event | category | flops | bytes accessed | tf_op | source)
XLA Modules:
  0.0 72.0 jit_solution(1659963631748543074)
XLA Ops:
  0.6 68.1 %shard_map.77 = (bf16[28,32,128]{2,1,0:T(8,128)(2,1)}, f32[256,1024]{1,0:T(8,128)}) custom-call(bf16[1024,128]{1,0:T(8,128)(2,1)} %bitcast.17, bf16[28,128,128]{2,1,0:T(8,128)(2,1)} %bitcast.16, bf16[7,128,128]{2,1,0:T(8,128)(2,1)} %bil_h.1, s32[8,4,128]{2,1,0:T(4,128)} %bitcast.19, s32[8,128]{1,0:T(8,128)} %bitcast.20, s32[512,8,128]{2,1,0:T(8,128)} %bitcast.13), custom_call_target="tpu_custom_call" | custom-call | tf_op jit(solution)/shard_map/pallas_call | solution.py:394
  68.7 0.0 copy-start
  68.7 2.4 %copy.8 = f32[32,8,8,128]{3,2,1,0:T(8,128)} copy(f32[32,8,8,128]{3,1,2,0:T(8,128)} %bitcast.15) | data formatting | bytes 2097152
  71.2 0.0 copy-done
  71.2 0.8 %bitcast_convert_fusion = f32[7,128,128]{2,1,0:T(8,128)} fusion(bf16[7,128,128]{2,1,0:T(8,128)(2,1)S(1)} %bitcast.18), kind=kLoop, calls=%fused_computation | loop fusion | flops 114688 | bytes 688128 | tf_op jit(solution)/shard_map/convert_element_type | solution.py:454
Async XLA Ops:
  68.7 2.4 %copy-start = (bf16[28,32,128]{2,1,0:T(8,128)(2,1)S(1)}, bf16[28,32,128]{2,1,0:T(8,128)(2,1)}, u32[]{:S(2)}) copy-start(bf16[28,32,128]{2,1,0:T(8,128)(2,1)} %get-tuple-element.4) | copy-start | bytes 688132

commit v2 on v1

--- a/solution.py
+++ b/solution.py
@@ -19,7 +19,7 @@
 NCH = 2
 RED = 28
 PAIR = {(i, j): p for p, (i, j) in enumerate((i, j) for i in range(F) for j in range(i + 1, F))}
-F32, BF16, I32 = jnp.float32, jnp.bfloat16, jnp.int32
+F32, BF16, I32, I16 = jnp.float32, jnp.bfloat16, jnp.int32, jnp.int16
 
 
 def dev(z, p):
@@ -30,8 +30,23 @@
     return lax.broadcasted_iota(I32, shape, dim)
 
 
+def bf(x):
+    return x.astype(F32).astype(BF16)
+
+
 def onehot(mask):
-    return jnp.where(mask, 1.0, 0.0).astype(BF16)
+    return jnp.where(mask, jnp.ones((), BF16), jnp.zeros((), BF16))
+
+
+def only(mask, x):
+    return jnp.where(mask, x, jnp.zeros((), BF16))
+
+
+def colsum(x):
+    acc = x[:16]
+    for i in range(16, x.shape[0], 16):
+        acc = acc + x[i : i + 16]
+    return jnp.sum(acc.astype(F32), axis=0, keepdims=True)
 
 
 def dot(a, b, ca=1, cb=0):
@@ -44,7 +59,7 @@
     pool, cot, bil, ids, lens, home,
     pf, up, proj, back, share,
     own, loc, live, m4, mall, dsend, drecv, cbuf,
-    vbuf, stage, got, amat, bmat,
+    vbuf, stage, got,
     w2, w3, w4, part,
     lsem, zs, zr, ms, mr, ds_, dr, ss, rr, ws, wr,
 ):
@@ -71,43 +86,49 @@
     def _(t):
         pl.semaphore_signal(bar, inc=1, device_id=dev((z + t) % NZ, me), device_id_type=MESH)
 
-    loads[0].wait()
-    perm = onehot(iota((128, 128), 1) == (iota((128, 128), 0) % 16) * F + iota((128, 128), 0) // 16)
-    x = jnp.concatenate([pool[pl.ds(g * 128, 128), :] for g in range(8)], axis=1)
-    y = dot(perm, x).astype(BF16)
-    for g in range(8):
-        for f in range(F):
-            pf[f, pl.ds(g * 16, 16), :] = y[f * 16 : f * 16 + 16, g * 128 : g * 128 + 128]
-    loads[1].wait()
-    for i in range(F - 1):
-        proj[i] = dot(pf[i], bil[i])
-    loads[2].wait()
-
-    @pl.loop(0, 8)
-    def _(r):
-        rows = pl.ds(pl.multiple_of(r * 16, 16), 16)
-        pj = [pf[j, rows, :].astype(F32) for j in range(F)]
+    with jax.named_scope("perm"):
+        loads[0].wait()
+        perm = jnp.where(iota((128, 128), 1) == (iota((128, 128), 0) % 16) * F + iota((128, 128), 0) // 16, 1.0, 0.0).astype(BF16)
+        x = jnp.concatenate([pool[pl.ds(g * 128, 128), :] for g in range(8)], axis=1)
+        y = dot(perm, x).astype(BF16)
+        for g in range(8):
+            for f in range(F):
+                pf[f, pl.ds(g * 16, 16), :] = y[f * 16 : f * 16 + 16, g * 128 : g * 128 + 128]
+    with jax.named_scope("proj"):
+        loads[1].wait()
         for i in range(F - 1):
-            run = cot[PAIR[i, i + 1], rows, :].astype(F32) * pj[i + 1]
-            for j in range(i + 2, F):
-                run = run + cot[PAIR[i, j], rows, :].astype(F32) * pj[j]
-            up[i, rows, :] = run.astype(BF16)
-
-    for i in range(F - 1):
-        back[i] = dot(up[i], bil[i], 1, 1)
-    for i in range(F - 1):
-        share[pl.ds(i * 128, 128), :] = dot(pf[i], up[i], 0, 0).astype(BF16)
-
-    @pl.loop(0, 8)
-    def _(r):
-        rows = pl.ds(pl.multiple_of(r * 16, 16), 16)
-        for i in range(F):
-            run = back[i, rows, :] if i < F - 1 else cot[PAIR[0, i], rows, :].astype(F32) * proj[0, rows, :]
-            for k in range(0 if i < F - 1 else 1, i):
-                run = run + cot[PAIR[k, i], rows, :].astype(F32) * proj[k, rows, :]
-            vbuf[0, pl.ds(pl.multiple_of(i * 128 + r * 16, 16), 16), :] = run.astype(BF16)
-
-    pl.semaphore_wait(bar, NP - 1 + NZ - 1)
+            proj[i] = dot(pf[i], bil[i])
+        loads[2].wait()
+
+    with jax.named_scope("upper"):
+        @pl.loop(0, 8)
+        def _(r):
+            rows = pl.ds(pl.multiple_of(r * 16, 16), 16)
+            pj = [pf[j, rows, :].astype(F32) for j in range(F)]
+            for i in range(F - 1):
+                run = cot[PAIR[i, i + 1], rows, :].astype(F32) * pj[i + 1]
+                for j in range(i + 2, F):
+                    run = run + cot[PAIR[i, j], rows, :].astype(F32) * pj[j]
+                up[i, rows, :] = run.astype(BF16)
+
+    with jax.named_scope("mm"):
+        for i in range(F - 1):
+            back[i] = dot(up[i], bil[i], 1, 1)
+        for i in range(F - 1):
+            share[pl.ds(i * 128, 128), :] = dot(pf[i], up[i], 0, 0).astype(BF16)
+
+    with jax.named_scope("fgrad"):
+        @pl.loop(0, 8)
+        def _(r):
+            rows = pl.ds(pl.multiple_of(r * 16, 16), 16)
+            for i in range(F):
+                run = back[i, rows, :] if i < F - 1 else cot[PAIR[0, i], rows, :].astype(F32) * proj[0, rows, :]
+                for k in range(0 if i < F - 1 else 1, i):
+                    run = run + cot[PAIR[k, i], rows, :].astype(F32) * proj[k, rows, :]
+                vbuf[0, pl.ds(pl.multiple_of(i * 128 + r * 16, 16), 16), :] = run.astype(BF16)
+
+    with jax.named_scope("barrier"):
+        pl.semaphore_wait(bar, NP - 1 + NZ - 1)
 
     half = ROWS // NCH
 
@@ -119,12 +140,10 @@
             device_id=dev(up_z if d == 0 else dn_z, me), device_id_type=MESH,
         )
 
-    def zcopy_wait(d, t, c):
-        zcopy(d, t, c).wait_recv()
-
-    for c in range(NCH):
-        for d in range(2):
-            zcopy(d, 1, c).start()
+    with jax.named_scope("zstart"):
+        for c in range(NCH):
+            for d in range(2):
+                zcopy(d, 1, c).start()
 
     def w2copy(r):
         return pltpu.make_async_remote_copy(
@@ -132,55 +151,61 @@
             device_id=dev(z, r), device_id_type=MESH,
         )
 
-    @pl.loop(0, NP)
-    def _(j):
-        r = me ^ j
-
-        @pl.when((r < RED) & (j > 0))
-        def _():
-            w2copy(r).start()
-
-    loads[3].wait()
-    loads[4].wait()
-    loads[5].wait()
-    hi_iota, lo_iota = iota((512, 128), 0), iota((128, 128), 0)
-    for f in range(F):
-        t = home[:, f, :]
-        table = jnp.concatenate([(t >> 8).astype(F32), (t & 255).astype(F32)], axis=1).astype(BF16)
-        idr = ids[f]
-        hi, lo = idr >> 7, idr & 127
-        oh = jnp.concatenate([onehot(hi_iota == hi[k : k + 1]) for k in range(BAG)], axis=1)
-        out = dot(table, oh, 0, 0)
-        for k in range(BAG):
-            mask = lo_iota == lo[k : k + 1]
-            cols = slice(k * 128, k * 128 + 128)
-            row = f * BAG + k
-            own[row : row + 1, :] = jnp.sum(jnp.where(mask, out[:128, cols], 0.0), axis=0, keepdims=True).astype(I32)
-            loc[row : row + 1, :] = jnp.sum(jnp.where(mask, out[128:, cols], 0.0), axis=0, keepdims=True)
-            live[row : row + 1, :] = jnp.where(lens[f : f + 1, :] > k, float(f + 1), 0.0)
-
-    upper_tri = jnp.concatenate(
-        [onehot(iota((256, 256), 0) < iota((256, 256), 1)), jnp.ones((256, 128), BF16)], axis=1
-    )
-    own_iota = iota((256, 256), 0)
-    o4_iota, rr_iota = iota((64, 256), 0), iota((128, 256), 0)
-    lane = (iota((1, 256), 1) % 128).astype(F32)
-
-    def rank_block(j, carry):
-        before, table = carry
-        two = lambda ref: jnp.concatenate([ref[pl.ds(2 * j, 1), :], ref[pl.ds(2 * j + 1, 1), :]], axis=1)
-        o = two(own)
-        hit = own_iota == o
-        res = dot(onehot(hit), upper_tri)
-        ahead = res[:, :256] + jnp.concatenate([before, before], axis=1)
-        rank = jnp.sum(jnp.where(hit, ahead, 0.0), axis=0, keepdims=True).astype(I32)
-        spot = rr_iota == (o & 3) * CAP + rank
-        pay = [jnp.where(spot, v, 0.0).astype(BF16) for v in (lane, two(live), two(loc))]
-        table = table + dot(onehot(o4_iota == (o >> 2)), jnp.concatenate(pay, axis=0), 1, 1)
-        return before + res[:, 256:], table
-
-    _, table = lax.fori_loop(0, 16, rank_block, (jnp.zeros((256, 128), F32), jnp.zeros((64, 384), F32)))
-    m4[...] = (table[:, :128] + 128.0 * table[:, 128:256] + 2048.0 * table[:, 256:]).astype(I32)
+    with jax.named_scope("w2start"):
+        @pl.loop(0, NP)
+        def _(j):
+            r = me ^ j
+
+            @pl.when((r < RED) & (j > 0))
+            def _():
+                w2copy(r).start()
+
+    with jax.named_scope("lookup"):
+        loads[3].wait()
+        loads[4].wait()
+        loads[5].wait()
+        hi_iota, lo_iota = iota((512, 128), 0).astype(I16), bf(iota((128, 128), 0))
+        for f in range(F):
+            t = home[pl.ds(f, 512, stride=F), :].T
+            table = bf(jnp.concatenate([t >> 8, t & 255], axis=0))
+            hi, lo = (ids[f] >> 7).astype(I16), bf(ids[f] & 127)
+            oh = jnp.concatenate([onehot(hi_iota == hi[k : k + 1]) for k in range(BAG)], axis=1)
+            out = dot(table, oh).astype(BF16)
+            for k in range(BAG):
+                mask = lo_iota == lo[k : k + 1]
+                cols = slice(k * 128, k * 128 + 128)
+                row = f * BAG + k
+                own[row : row + 1, :] = colsum(only(mask, out[:128, cols])).astype(I32)
+                loc[row : row + 1, :] = colsum(only(mask, out[128:, cols]))
+                live[row : row + 1, :] = jnp.where(lens[f : f + 1, :] > k, float(f + 1), 0.0)
+
+    with jax.named_scope("rank"):
+        tri = jnp.where(iota((256, 256), 0) < iota((256, 256), 1), 1.0, 0.0).astype(BF16)
+        tri = jnp.concatenate([tri, jnp.ones((256, 128), BF16)], axis=1)
+        own_iota, o4_iota, rr_iota = bf(iota((256, 128), 0)), bf(iota((64, 128), 0)), bf(iota((128, 128), 0))
+        lane = bf(iota((1, 128), 1) + 1)
+        o = own[...]
+        o_b, o4_b, oc_b = bf(o), bf(o >> 2), bf((o & 3) * CAP)
+        loc_b, live_b = loc[...].astype(BF16), live[...].astype(BF16)
+        before = jnp.zeros((256, 128), BF16)
+        table, lhs, rhs = jnp.zeros((128, 256), F32), [], []
+        for j in range(16):
+            hit = [own_iota == o_b[r : r + 1] for r in (2 * j, 2 * j + 1)]
+            res = dot(jnp.concatenate([onehot(h) for h in hit], axis=1), tri).astype(BF16)
+            for n in range(2):
+                r = slice(2 * j + n, 2 * j + n + 1)
+                rank = colsum(only(hit[n], res[:, n * 128 : n * 128 + 128] + before))
+                spot = rr_iota == oc_b[r] + rank.astype(BF16)
+                four = o4_iota == o4_b[r]
+                rhs.append(jnp.concatenate([only(spot, lane), only(spot, loc_b[r])], axis=0))
+                lhs.append(jnp.concatenate([onehot(four), only(four, live_b[r])], axis=0))
+            before = before + res[:, 256:]
+            if j % 4 == 3:
+                table = table + dot(jnp.concatenate(lhs, axis=1), jnp.concatenate(rhs, axis=1), 1, 1)
+                lhs, rhs = [], []
+        b1 = table[:64, :128]
+        f1 = jnp.round(table[64:, :128] / jnp.maximum(b1, 1.0))
+        m4[...] = jnp.where(b1 > 0, (b1 - 1.0) + 128.0 * f1 + 2048.0 * table[:64, 128:], 0.0).astype(I32)
     mall[0] = m4[pl.ds(pl.multiple_of(z * 8, 8), 8), :]
 
     def mcopy(t):
@@ -193,13 +218,13 @@
     def _(t):
         mcopy(t).start()
 
-    lane128 = iota((128, 128), 1)
+    lane128 = iota((128, 128), 1).astype(I16)
 
     def gather(idx):
         for pq in range(8):
             row = mall[idx, pl.ds(pq, 1), :] & 2047
-            col = jnp.broadcast_to(row, (128, 128)).T
-            g = jnp.concatenate([onehot(col == lane128 + 128 * (f + 1)) for f in range(F)], axis=1)
+            col = jnp.broadcast_to(row, (128, 128)).T.astype(I16)
+            g = jnp.concatenate([onehot(col == lane128 + jnp.asarray(128 * (f + 1), I16)) for f in range(F)], axis=1)
             rows = dot(g, vbuf[idx]).astype(BF16)
             stage[idx, pl.ds(pq * 4, 4)] = rows.reshape(4, CAP, D)
 
@@ -215,22 +240,23 @@
         def _(j):
             xycopy(idx, me ^ j).start()
 
-    q_iota = iota((256, 128), 0)
+    q_iota = bf(iota((256, 128), 0))
 
     def accumulate(idx):
         peers = got.at[idx, pl.ds(0, NP - 1)]
-        pltpu.make_async_copy(peers, peers, rr.at[idx]).wait()
+        with jax.named_scope("waitxy"):
+            pltpu.make_async_copy(peers, peers, rr.at[idx]).wait()
         code = cbuf[idx]
-        fcode = (code >> 7) & 15
-        lcode = code >> 11
+        field, local = ((code >> 7) & 15).astype(F32), bf(code >> 11)
+        lhs, rhs = [], []
         for g in range(8):
-            fcol = jnp.broadcast_to(fcode[g : g + 1, :].astype(F32), (128, 128)).T.astype(BF16)
+            fcol = jnp.broadcast_to(field[g : g + 1, :], (128, 128)).T.astype(BF16)
             v = got[idx, pl.ds(g * 4, 4)].reshape(128, D)
-            rows = pl.ds(g * 128, 128)
-            for f in range(F):
-                bmat[rows, f * D : f * D + D] = jnp.where(fcol == jnp.asarray(f + 1, BF16), v, jnp.zeros_like(v))
-            amat[:, g * 128 : g * 128 + 128] = onehot(q_iota == lcode[g : g + 1, :])
-        acc_o[...] += dot(amat[...], bmat[...])
+            rhs.append(jnp.concatenate([only(fcol == jnp.asarray(f + 1, BF16), v) for f in range(F)], axis=1))
+            lhs.append(onehot(q_iota == local[g : g + 1, :]))
+            if g % 4 == 3:
+                acc_o[...] += dot(jnp.concatenate(lhs, axis=1), jnp.concatenate(rhs, axis=0))
+                lhs, rhs = [], []
 
     def dcopy(q):
         return pltpu.make_async_remote_copy(
@@ -238,8 +264,6 @@
         )
 
     def targets_out():
-        many = mall.at[pl.ds(1, NZ - 1)]
-        pltpu.make_async_copy(many, many, mr).wait()
         mine = iota((8, 128), 1) // CAP == me % 4
         for pq in range(8):
             x = mall[:, pq, :]
@@ -303,51 +327,72 @@
 
     acc_o[...] = jnp.zeros_like(acc_o)
 
+    def pass_on(t, c):
+        for d in range(2):
+            with jax.named_scope("waitz"):
+                zcopy(d, t, c).wait_recv()
+
+            @pl.when((t < 3) | ((c < NCH // 2) == (d == 0)))
+            def _():
+                zcopy(d, t + 1, c).start()
+
     @pl.loop(0, 9)
     def _(n):
         t = (n + 1) // 2
 
         @pl.when((n % 2 == 1) & (n < 7))
         def _():
-            for c in range(NCH):
-                for d in range(2):
-                    zcopy_wait(d, t, c)
-
-                    @pl.when((t < 3) | ((c < NCH // 2) == (d == 0)))
-                    def _():
-                        zcopy(d, t + 1, c).start()
+            for c in range(NCH // 2, NCH):
+                pass_on(t, c)
 
         @pl.when(n == 7)
         def _():
             for c in range(NCH // 2):
-                zcopy_wait(0, 4, c)
-                zcopy_wait(1, 4, c + NCH // 2)
-
-        @pl.when(n == 1)
-        def _():
-            targets_out()
-            weight_add()
+                zcopy(0, 4, c).wait_recv()
+                zcopy(1, 4, c + NCH // 2).wait_recv()
 
         @pl.when(n < 8)
         def _():
-            gather(at(n))
-            send(at(n))
+            @pl.when(n == 1)
+            def _():
+                with jax.named_scope("waitm"):
+                    many = mall.at[pl.ds(1, NZ - 1)]
+                    pltpu.make_async_copy(many, many, mr).wait()
+
+            with jax.named_scope("gather"):
+                gather(at(n))
+            with jax.named_scope("send"):
+                send(at(n))
+
+        @pl.when((n % 2 == 0) & (n < 6))
+        def _():
+            for c in range(NCH // 2):
+                pass_on(t + 1, c)
 
         @pl.when(n == 2)
         def _():
-            targets_in()
+            with jax.named_scope("targets_out"):
+                targets_out()
+            with jax.named_scope("weight_add"):
+                weight_add()
 
         @pl.when(n == 4)
         def _():
-            weight_spread()
-
-        @pl.when(n >= 2)
-        def _():
-            accumulate(at(n - 1))
-
-        @pl.when(n == 2)
-        def _():
-            accumulate(0)
+            with jax.named_scope("targets_in"):
+                targets_in()
+
+        @pl.when(n == 5)
+        def _():
+            with jax.named_scope("weight_spread"):
+                weight_spread()
+
+        first = jnp.where(n <= 4, 0, jnp.where(n <= 6, n - 4, jnp.where(n == 7, 4, 5)))
+        last = jnp.where(n < 4, 0, jnp.where(n <= 5, n - 3, jnp.where(n == 6, 4, jnp.where(n == 7, 5, 8))))
+
+        @pl.loop(first, last)
+        def _(m):
+            with jax.named_scope("acc"):
+                accumulate(at(m))
 
     @pl.when(me < RED)
     def _():
@@ -405,7 +450,7 @@
             pltpu.VMEM((F - 1, D, D), BF16),
             pltpu.VMEM((F, BAG, TOK), I32),
             pltpu.VMEM((F, TOK), I32),
-            pltpu.VMEM((512, F, 128), I32),
+            pltpu.VMEM((512 * F, 128), I32),
             pltpu.VMEM((F, TOK, D), BF16),
             pltpu.VMEM((F - 1, TOK, D), BF16),
             pltpu.VMEM((F - 1, TOK, D), F32),
@@ -422,8 +467,6 @@
             pltpu.VMEM((NZ, ROWS, D), BF16),
             pltpu.VMEM((NZ, NP, CAP, D), BF16),
             pltpu.VMEM((NZ, NP, CAP, D), BF16),
-            pltpu.VMEM((256, 1024), BF16),
-            pltpu.VMEM((1024, F * D), BF16),
             pltpu.VMEM((NP, 32, D), BF16),
             pltpu.VMEM((NZ, 32, D), F32),
             pltpu.VMEM((RED, 32, D), BF16),
@@ -449,7 +492,7 @@
         bilinear,
         bag_ids.transpose(1, 2, 0),
         bag_lens.transpose(1, 0),
-        row_home.reshape(F, 512, 128).transpose(1, 0, 2),
+        row_home.reshape(F, 512, 128).transpose(1, 0, 2).reshape(512 * F, 128),
     )
     return wg.reshape(F - 1, D, D).astype(F32), acc.reshape(256, F, D)
 

time: 72.1 us -> 56.7 us (0.79)
  Pallas kernels: 68.1 us -> 52.7 us
    pallas_call x1, Pallas kernels: 68.1 us -> 52.7 us  [on_device(): pl.pallas_call(body, out_shape=(jax.ShapeDtypeStruct((RED, 32, D), BF16),...]
where the time goes in v2:
time: 56.7 us; the launch traced here: 56.6 us
  Pallas kernels  52.7 us (93%)
  local copies, waits for them, and re-layouts  2.44 us (4%)
  other arithmetic  0.8 us (1%)
  between operations  0.65 us (1%)
    pallas_call x1, Pallas kernels, on_device(): pl.pallas_call(body, out_shape=(jax.ShapeDtypeStruct((RED, 32, D), BF16),...  52.7 us
    unnamed x3, local copies, waits for them, and re-layouts  2.44 us

profile of v2, /device:TPU:1, one launch (start us, length us, event | category | flops | bytes accessed | tf_op | source)
XLA Modules:
  0.0 56.6 jit_solution(16790147321477804293)
XLA Ops:
  0.6 52.7 %shard_map.77 = (bf16[28,32,128]{2,1,0:T(8,128)(2,1)}, f32[256,1024]{1,0:T(8,128)}) custom-call(bf16[1024,128]{1,0:T(8,128)(2,1)} %bitcast.19, bf16[28,128,128]{2,1,0:T(8,128)(2,1)} %bitcast.18, bf16[7,128,128]{2,1,0:T(8,128)(2,1)} %bil_h.1, s32[8,4,128]{2,1,0:T(4,128)} %bitcast.21, s32[8,128]{1,0:T(8,128)} %bitcast.22, s32[4096,128]{1,0:T(8,128)} %bitcast.15), custom_call_target="tpu_custom_call" | custom-call | tf_op jit(solution)/shard_map/pallas_call | solution.py:439
  53.3 0.0 copy-start
  53.4 2.4 %copy.8 = f32[32,8,8,128]{3,2,1,0:T(8,128)} copy(f32[32,8,8,128]{3,1,2,0:T(8,128)} %bitcast.17) | data formatting | bytes 2097152
  55.8 0.0 copy-done
  55.8 0.8 %bitcast_convert_fusion = f32[7,128,128]{2,1,0:T(8,128)} fusion(bf16[7,128,128]{2,1,0:T(8,128)(2,1)S(1)} %bitcast.20), kind=kLoop, calls=%fused_computation | loop fusion | flops 114688 | bytes 688128 | tf_op jit(solution)/shard_map/convert_element_type | solution.py:497
Async XLA Ops:
  53.3 2.4 %copy-start = (bf16[28,32,128]{2,1,0:T(8,128)(2,1)S(1)}, bf16[28,32,128]{2,1,0:T(8,128)(2,1)}, u32[]{:S(2)}) copy-start(bf16[28,32,128]{2,1,0:T(8,128)(2,1)} %get-tuple-element.4) | copy-start | bytes 688132

commit v3 on v2

--- a/solution.py
+++ b/solution.py
@@ -53,14 +53,54 @@
     return lax.dot_general(a, b, (((ca,), (cb,)), ((), ())), preferred_element_type=F32)
 
 
+def wait_all(ref, sem):
+    pltpu.make_async_copy(ref, ref, sem).wait()
+
+
+def add_slots(code, rows, acc):
+    field, local = (code & 15).astype(F32), bf(code >> 4)
+    q_iota = bf(iota((256, 128), 0))
+    lhs, rhs = [], []
+    for g in range(8):
+        fcol = jnp.broadcast_to(field[g : g + 1, :], (128, 128)).T.astype(BF16)
+        v = rows[pl.ds(g * 4, 4)].reshape(128, D)
+        rhs.append(jnp.concatenate([only(fcol == jnp.asarray(f + 1, BF16), v) for f in range(F)], axis=1))
+        lhs.append(onehot(q_iota == local[g : g + 1, :]))
+        if g % 4 == 3:
+            acc[...] += dot(jnp.concatenate(lhs, axis=1), jnp.concatenate(rhs, axis=0))
+            lhs, rhs = [], []
+
+
+def finish(acc_h, got_h, code_h, w4_h, wg_o, tab_o, acc, got, code, w4, wg, part, table, sem):
+    loads = [pltpu.make_async_copy(a, b, sem.at[n]) for n, (a, b) in enumerate([(got_h, got), (code_h, code), (w4_h, w4), (acc_h, acc)])]
+    for c in loads:
+        c.start()
+    part[...] = jnp.zeros_like(part)
+    loads[0].wait()
+    loads[1].wait()
+    add_slots(code[...], got, part)
+    loads[2].wait()
+    wg[...] = w4[...].astype(F32)
+    wg_out = pltpu.make_async_copy(wg, wg_o, sem.at[4])
+    wg_out.start()
+    loads[3].wait()
+    for f in range(F):
+        cols = slice(f * D, f * D + D)
+        table[pl.ds(f, 256, stride=F), :] = acc[:, cols] + part[:, cols]
+    table_out = pltpu.make_async_copy(table, tab_o, sem.at[5])
+    table_out.start()
+    wg_out.wait()
+    table_out.wait()
+
+
 def body(
     pool_h, cot_h, bil_h, ids_h, lens_h, home_h,
-    wg_o, acc_o,
+    acc_o, got_o, code_o, w4_o,
     pool, cot, bil, ids, lens, home,
     pf, up, proj, back, share,
     own, loc, live, m4, mall, dsend, drecv, cbuf,
     vbuf, stage, got,
-    w2, w3, w4, part,
+    acc, w2, w3, w4, part, done,
     lsem, zs, zr, ms, mr, ds_, dr, ss, rr, ws, wr,
 ):
     gx, gy = lax.axis_index("gx"), lax.axis_index("gy")
@@ -126,39 +166,6 @@
                 for k in range(0 if i < F - 1 else 1, i):
                     run = run + cot[PAIR[k, i], rows, :].astype(F32) * proj[k, rows, :]
                 vbuf[0, pl.ds(pl.multiple_of(i * 128 + r * 16, 16), 16), :] = run.astype(BF16)
-
-    with jax.named_scope("barrier"):
-        pl.semaphore_wait(bar, NP - 1 + NZ - 1)
-
-    half = ROWS // NCH
-
-    def zcopy(d, t, c):
-        src, dst = (t - 1, t) if d == 0 else ((8 - (t - 1)) % 8, 8 - t)
-        rows = pl.ds(c * half, half)
-        return pltpu.make_async_remote_copy(
-            vbuf.at[src, rows], vbuf.at[dst, rows], zs.at[d, t - 1, c], zr.at[d, t - 1, c],
-            device_id=dev(up_z if d == 0 else dn_z, me), device_id_type=MESH,
-        )
-
-    with jax.named_scope("zstart"):
-        for c in range(NCH):
-            for d in range(2):
-                zcopy(d, 1, c).start()
-
-    def w2copy(r):
-        return pltpu.make_async_remote_copy(
-            share.at[pl.ds(pl.multiple_of(r * 32, 32), 32)], w2.at[me], ws.at[0], wr.at[0],
-            device_id=dev(z, r), device_id_type=MESH,
-        )
-
-    with jax.named_scope("w2start"):
-        @pl.loop(0, NP)
-        def _(j):
-            r = me ^ j
-
-            @pl.when((r < RED) & (j > 0))
-            def _():
-                w2copy(r).start()
 
     with jax.named_scope("lookup"):
         loads[3].wait()
@@ -178,6 +185,44 @@
                 own[row : row + 1, :] = colsum(only(mask, out[:128, cols])).astype(I32)
                 loc[row : row + 1, :] = colsum(only(mask, out[128:, cols]))
                 live[row : row + 1, :] = jnp.where(lens[f : f + 1, :] > k, float(f + 1), 0.0)
+
+    with jax.named_scope("barrier"):
+        pl.semaphore_wait(bar, NP - 1 + NZ - 1)
+
+    half = ROWS // NCH
+
+    def zcopy(d, t, c):
+        src, dst = (t - 1, t) if d == 0 else ((8 - (t - 1)) % 8, 8 - t)
+        rows = pl.ds(c * half, half)
+        return pltpu.make_async_remote_copy(
+            vbuf.at[src, rows], vbuf.at[dst, rows], zs.at[d, t - 1, c], zr.at[d, t - 1, c],
+            device_id=dev(up_z if d == 0 else dn_z, me), device_id_type=MESH,
+        )
+
+    def first_hop(pieces):
+        for c in pieces:
+            for d in range(2):
+                zcopy(d, 1, c).start()
+
+    first_hop(range(NCH // 2))
+
+    def w2copy(r):
+        return pltpu.make_async_remote_copy(
+            share.at[pl.ds(pl.multiple_of(r * 32, 32), 32)], w2.at[me], ws.at[0], wr.at[0],
+            device_id=dev(z, r), device_id_type=MESH,
+        )
+
+    def shares_out():
+        @pl.loop(0, NP)
+        def _(j):
+            r = me ^ j
+
+            @pl.when((r < RED) & (j > 0))
+            def _():
+                w2copy(r).start()
+
+    with jax.named_scope("shares_out"):
+        shares_out()
 
     with jax.named_scope("rank"):
         tri = jnp.where(iota((256, 256), 0) < iota((256, 256), 1), 1.0, 0.0).astype(BF16)
@@ -211,12 +256,14 @@
     def mcopy(t):
         to = (z + t) % NZ
         return pltpu.make_async_remote_copy(
-            m4.at[pl.ds(pl.multiple_of(to * 8, 8), 8)], mall.at[t], ms, mr, device_id=dev(to, me), device_id_type=MESH
+            m4.at[pl.ds(pl.multiple_of(to * 8, 8), 8)], mall.at[t], ms, mr.at[t], device_id=dev(to, me), device_id_type=MESH
         )
 
     @pl.loop(1, NZ)
     def _(t):
         mcopy(t).start()
+
+    first_hop(range(NCH // 2, NCH))
 
     lane128 = iota((128, 128), 1).astype(I16)
 
@@ -240,23 +287,22 @@
         def _(j):
             xycopy(idx, me ^ j).start()
 
-    q_iota = bf(iota((256, 128), 0))
+    def last_own():
+        return pltpu.make_async_copy(stage.at[4, me], got_o.at[me], lsem.at[6])
+
+    def send_last():
+        last_own().start()
+
+        @pl.loop(1, NP)
+        def _(j):
+            pltpu.make_async_remote_copy(
+                stage.at[4, me ^ j], got_o.at[me], ss.at[4], rr.at[4], device_id=dev(z, me ^ j), device_id_type=MESH
+            ).start()
 
     def accumulate(idx):
-        peers = got.at[idx, pl.ds(0, NP - 1)]
         with jax.named_scope("waitxy"):
-            pltpu.make_async_copy(peers, peers, rr.at[idx]).wait()
-        code = cbuf[idx]
-        field, local = ((code >> 7) & 15).astype(F32), bf(code >> 11)
-        lhs, rhs = [], []
-        for g in range(8):
-            fcol = jnp.broadcast_to(field[g : g + 1, :], (128, 128)).T.astype(BF16)
-            v = got[idx, pl.ds(g * 4, 4)].reshape(128, D)
-            rhs.append(jnp.concatenate([only(fcol == jnp.asarray(f + 1, BF16), v) for f in range(F)], axis=1))
-            lhs.append(onehot(q_iota == local[g : g + 1, :]))
-            if g % 4 == 3:
-                acc_o[...] += dot(jnp.concatenate(lhs, axis=1), jnp.concatenate(rhs, axis=0))
-                lhs, rhs = [], []
+            wait_all(got.at[idx, pl.ds(0, NP - 1)], rr.at[idx])
+        add_slots(cbuf[idx], got.at[idx], acc)
 
     def dcopy(q):
         return pltpu.make_async_remote_copy(
@@ -264,12 +310,14 @@
         )
 
     def targets_out():
+        for t in range(2, NZ - 1):
+            mcopy(t).wait_recv()
         mine = iota((8, 128), 1) // CAP == me % 4
         for pq in range(8):
-            x = mall[:, pq, :]
+            x = mall[:, pq, :] >> 7
             for s in range(4):
                 y = pltpu.roll(x, s * CAP, 1) if s else x
-                dsend[pq * 4 + (me % 4 + 4 - s) % 4] = jnp.where(mine, y, 0)
+                dsend[pq * 4 + (me % 4 + 4 - s) % 4] = jnp.where(mine, y, 0).astype(I16)
         drecv[me] = dsend[me]
 
         @pl.loop(1, NP)
@@ -280,52 +328,86 @@
         many = drecv.at[pl.ds(0, NP - 1)]
         pltpu.make_async_copy(many, many, dr).wait()
         for g in range(8):
-            cbuf[:, g, :] = drecv[4 * g] + drecv[4 * g + 1] + drecv[4 * g + 2] + drecv[4 * g + 3]
+            cbuf[:, g, :] = sum(drecv[4 * g + n].astype(I32) for n in range(4))
 
     def w3copy(t):
-        return pltpu.make_async_remote_copy(
-            part, w3.at[z], ws.at[1], wr.at[1], device_id=dev((z + t) % NZ, me), device_id_type=MESH
+        to = (z + t) % NZ
+        return pltpu.make_async_remote_copy(
+            part.at[to], w3.at[z], ws.at[1], wr.at[1], device_id=dev(to, me), device_id_type=MESH
+        )
+
+    def w3back(t):
+        return pltpu.make_async_remote_copy(
+            done.at[z], done.at[z], ws.at[2], wr.at[2], device_id=dev((z + t) % NZ, me), device_id_type=MESH
         )
 
     def w4copy(q):
-        return pltpu.make_async_remote_copy(
-            w4.at[me], w4.at[me], ws.at[2], wr.at[2], device_id=dev(z, q), device_id_type=MESH
-        )
+        mine = w4.at[me // 2, me % 2]
+        return pltpu.make_async_remote_copy(
+            mine, mine, ws.at[3], wr.at[3], device_id=dev(z, q), device_id_type=MESH
+        )
+
+    def w4side():
+        mine = w4.at[:, me % 2]
+        return pltpu.make_async_remote_copy(
+            mine, mine, ws.at[4], wr.at[4], device_id=dev(z, me ^ 1), device_id_type=MESH
+        )
+
+    adder = me < RED
 
     def weight_add():
-        @pl.when(me < RED)
-        def _():
-            peers = w2.at[pl.ds(0, NP - 1)]
+        @pl.when(adder)
+        def _():
             w2[me] = share[pl.ds(pl.multiple_of(me * 32, 32), 32), :]
-            pltpu.make_async_copy(peers, peers, wr.at[0]).wait()
+            wait_all(w2.at[pl.ds(0, NP - 1)], wr.at[0])
             total = w2[0].astype(F32)
             for i in range(1, NP):
                 total = total + w2[i].astype(F32)
-            part[...] = total
-            w3[z] = total
+            part[...] = total.reshape(NZ, 4, D)
+            w3[z] = part[z]
 
             @pl.loop(1, NZ)
             def _(t):
                 w3copy(t).start()
 
-    def weight_spread():
-        @pl.when(me < RED)
-        def _():
-            peers = w3.at[pl.ds(0, NZ - 1)]
-            pltpu.make_async_copy(peers, peers, wr.at[1]).wait()
+    def weight_column():
+        @pl.when(adder)
+        def _():
+            wait_all(w3.at[pl.ds(0, NZ - 1)], wr.at[1])
             total = w3[0]
             for i in range(1, NZ):
                 total = total + w3[i]
-            w4[me] = total.astype(BF16)
-
-            @pl.loop(1, NP)
+            done[z] = total
+
+            @pl.loop(1, NZ)
+            def _(t):
+                w3back(t).start()
+
+    def weight_spread():
+        @pl.when(adder)
+        def _():
+            wait_all(done.at[pl.ds(0, NZ - 1)], wr.at[2])
+            w4[me // 2, me % 2] = done[...].reshape(32, D).astype(BF16)
+
+            @pl.loop(1, NP // 2)
             def _(j):
-                w4copy(me ^ j).start()
+                w4copy(me ^ (2 * j)).start()
+
+    def weight_side():
+        @pl.when(adder)
+        def _():
+            wait_all(w4.at[pl.ds(0, RED // 2 - 1), 0], wr.at[3])
+
+        @pl.when(me >= RED)
+        def _():
+            wait_all(w4.at[:, 0], wr.at[3])
+
+        w4side().start()
 
     def at(n):
         return jnp.where(n == 7, 4, jnp.where(n % 2 == 1, (n + 1) // 2, (8 - n // 2) % 8))
 
-    acc_o[...] = jnp.zeros_like(acc_o)
+    acc[...] = jnp.zeros_like(acc)
 
     def pass_on(t, c):
         for d in range(2):
@@ -353,16 +435,24 @@
 
         @pl.when(n < 8)
         def _():
-            @pl.when(n == 1)
+            @pl.when((n == 1) | (n == 2))
             def _():
                 with jax.named_scope("waitm"):
-                    many = mall.at[pl.ds(1, NZ - 1)]
-                    pltpu.make_async_copy(many, many, mr).wait()
+                    mcopy(at(n)).wait_recv()
 
             with jax.named_scope("gather"):
                 gather(at(n))
-            with jax.named_scope("send"):
-                send(at(n))
+
+            @pl.when(n < 7)
+            def _():
+                with jax.named_scope("send"):
+                    send(at(n))
+
+            @pl.when(n == 7)
+            def _():
+                with jax.named_scope("send"):
+                    send_last()
+
 
         @pl.when((n % 2 == 0) & (n < 6))
         def _():
@@ -373,9 +463,17 @@
         def _():
             with jax.named_scope("targets_out"):
                 targets_out()
+
+        @pl.when(n == 1)
+        def _():
             with jax.named_scope("weight_add"):
                 weight_add()
 
+        @pl.when(n == 3)
+        def _():
+            with jax.named_scope("weight_column"):
+                weight_column()
+
         @pl.when(n == 4)
         def _():
             with jax.named_scope("targets_in"):
@@ -386,64 +484,67 @@
             with jax.named_scope("weight_spread"):
                 weight_spread()
 
+        @pl.when(n == 8)
+        def _():
+            with jax.named_scope("weight_side"):
+                weight_side()
+
         first = jnp.where(n <= 4, 0, jnp.where(n <= 6, n - 4, jnp.where(n == 7, 4, 5)))
-        last = jnp.where(n < 4, 0, jnp.where(n <= 5, n - 3, jnp.where(n == 6, 4, jnp.where(n == 7, 5, 8))))
+        last = jnp.where(n < 4, 0, jnp.where(n <= 5, n - 3, jnp.where(n == 6, 4, jnp.where(n == 7, 5, 7))))
 
         @pl.loop(first, last)
         def _(m):
             with jax.named_scope("acc"):
                 accumulate(at(m))
 
-    @pl.when(me < RED)
-    def _():
-        peers = w4.at[pl.ds(0, RED - 1)]
-        pltpu.make_async_copy(peers, peers, wr.at[2]).wait()
-
-    @pl.when(me >= RED)
-    def _():
-        pltpu.make_async_copy(w4, w4, wr.at[2]).wait()
-
-    wg_o[...] = w4[...]
+    w4side().wait()
+    outs = [
+        pltpu.make_async_copy(a, b, lsem.at[n])
+        for n, (a, b) in enumerate([(acc, acc_o), (cbuf.at[4], code_o), (w4, w4_o)])
+    ]
+    for c in outs:
+        c.start()
     for t in range(1, 5):
         for d in range(2):
             for c in range(NCH):
                 if t < 4 or (c < NCH // 2) == (d == 0):
                     zcopy(d, t, c).wait_send()
-    many = mall.at[pl.ds(0, NZ - 1)]
-    pltpu.make_async_copy(many, many, ms).wait()
-    many = dsend.at[pl.ds(0, NP - 1)]
-    pltpu.make_async_copy(many, many, ds_).wait()
+    wait_all(mall.at[pl.ds(0, NZ - 1)], ms)
+    wait_all(dsend.at[pl.ds(0, NP - 1)], ds_)
     for k in range(8):
-        many = stage.at[k, pl.ds(0, NP - 1)]
-        pltpu.make_async_copy(many, many, ss.at[k]).wait()
-
-    @pl.when(me < RED)
+        wait_all(stage.at[k, pl.ds(0, NP - 1)], ss.at[k])
+
+    @pl.when(adder)
     def _():
-        many = w2.at[pl.ds(0, RED - 1)]
-        pltpu.make_async_copy(many, many, ws.at[0]).wait()
-        many = w3.at[pl.ds(0, NZ - 1)]
-        pltpu.make_async_copy(many, many, ws.at[1]).wait()
-        many = w2.at[pl.ds(0, NP - 1)]
-        pltpu.make_async_copy(many, many, ws.at[2]).wait()
+        wait_all(w2.at[pl.ds(0, RED - 1)], ws.at[0])
+        wait_all(w3.at[pl.ds(0, NZ - 1)], ws.at[1])
+        wait_all(done.at[pl.ds(0, NZ - 1)], ws.at[2])
+        wait_all(w2.at[pl.ds(0, NP // 2 - 1)], ws.at[3])
 
     @pl.when(me >= RED)
     def _():
-        many = w2.at[pl.ds(0, RED)]
-        pltpu.make_async_copy(many, many, ws.at[0]).wait()
+        wait_all(w2.at[pl.ds(0, RED)], ws.at[0])
+
+    for c in outs:
+        c.wait()
+    last_own().wait()
+    with jax.named_scope("waitxy"):
+        wait_all(got_o.at[pl.ds(0, NP - 1)], rr.at[4])
 
 
 def on_device(pooled, cotangent, bilinear, bag_ids, bag_lens, row_home):
     any_ = pl.BlockSpec(memory_space=pl.ANY)
-    vm = pl.BlockSpec(memory_space=pltpu.VMEM)
     dma = pltpu.SemaphoreType.DMA
-    wg, acc = pl.pallas_call(
+    acc, got, code, w4 = pl.pallas_call(
         body,
         out_shape=(
-            jax.ShapeDtypeStruct((RED, 32, D), BF16),
             jax.ShapeDtypeStruct((256, F * D), F32),
+            jax.ShapeDtypeStruct((NP, CAP, D), BF16),
+            jax.ShapeDtypeStruct((8, 128), I32),
+            jax.ShapeDtypeStruct((RED // 2, 2, 32, D), BF16),
         ),
         in_specs=[any_] * 6,
-        out_specs=(vm, vm),
+        out_specs=[any_] * 4,
         scratch_shapes=[
             pltpu.VMEM((ROWS, D), BF16),
             pltpu.VMEM((28, TOK, D), BF16),
@@ -461,27 +562,29 @@
             pltpu.VMEM((F * BAG, 128), F32),
             pltpu.VMEM((64, 128), I32),
             pltpu.VMEM((NZ, 8, 128), I32),
-            pltpu.VMEM((NP, 8, 128), I32),
-            pltpu.VMEM((NP, 8, 128), I32),
+            pltpu.VMEM((NP, 8, 128), I16),
+            pltpu.VMEM((NP, 8, 128), I16),
             pltpu.VMEM((NZ, 8, 128), I32),
             pltpu.VMEM((NZ, ROWS, D), BF16),
             pltpu.VMEM((NZ, NP, CAP, D), BF16),
             pltpu.VMEM((NZ, NP, CAP, D), BF16),
+            pltpu.VMEM((256, F * D), F32),
             pltpu.VMEM((NP, 32, D), BF16),
-            pltpu.VMEM((NZ, 32, D), F32),
-            pltpu.VMEM((RED, 32, D), BF16),
-            pltpu.VMEM((32, D), F32),
-            dma((6,)),
+            pltpu.VMEM((NZ, 4, D), F32),
+            pltpu.VMEM((RED // 2, 2, 32, D), BF16),
+            pltpu.VMEM((NZ, 4, D), F32),
+            pltpu.VMEM((NZ, 4, D), F32),
+            dma((7,)),
             dma((2, 4, NCH)),
             dma((2, 4, NCH)),
             dma,
-            dma,
+            dma((NZ,)),
             dma,
             dma,
             dma((8,)),
             dma((8,)),
-            dma((3,)),
-            dma((3,)),
+            dma((5,)),
+            dma((5,)),
         ],
         compiler_params=pltpu.CompilerParams(
             collective_id=0, has_side_effects=True, vmem_limit_bytes=60 * 2**20
@@ -494,7 +597,27 @@
         bag_lens.transpose(1, 0),
         row_home.reshape(F, 512, 128).transpose(1, 0, 2).reshape(512 * F, 128),
     )
-    return wg.reshape(F - 1, D, D).astype(F32), acc.reshape(256, F, D)
+    wg, table = pl.pallas_call(
+        finish,
+        out_shape=(
+            jax.ShapeDtypeStruct(((F - 1) * D, D), F32),
+            jax.ShapeDtypeStruct((256 * F, D), F32),
+        ),
+        in_specs=[any_] * 4,
+        out_specs=[any_] * 2,
+        scratch_shapes=[
+            pltpu.VMEM((256, F * D), F32),
+            pltpu.VMEM((NP, CAP, D), BF16),
+            pltpu.VMEM((8, 128), I32),
+            pltpu.VMEM(((F - 1) * D, D), BF16),
+            pltpu.VMEM(((F - 1) * D, D), F32),
+            pltpu.VMEM((256, F * D), F32),
+            pltpu.VMEM((256 * F, D), F32),
+            dma((6,)),
+        ],
+        compiler_params=pltpu.CompilerParams(vmem_limit_bytes=60 * 2**20),
+    )(acc, got, code, w4.reshape((F - 1) * D, D))
+    return wg.reshape(F - 1, D, D), table.reshape(256, F, D)
 
 
 def solution(mesh):

time: 56.7 us -> 51.6 us (0.910)
  local copies, waits for them, and re-layouts: 2.44 us -> 0 us
  Pallas kernels: 52.7 us -> 50.9 us
  other arithmetic: 0.8 us -> 0 us
    unnamed x3 -> x0, local copies, waits for them, and re-layouts: 2.44 us -> none
    pallas_call x1 -> x2, Pallas kernels: 52.7 us -> 50.9 us  [the longest x1 47.7 us: on_device(): pl.pallas_call(body, out_shape=(jax.ShapeDtypeStruct((256, F * D), F32),...]
    convert_element_type x1 -> x0, other arithmetic: 0.8 us -> none  [on_device(): return (wg.reshape(F - 1, D, D).astype(F32), acc.reshape(256, F, D))]
where the time goes in v3:
time: 51.6 us; the launch traced here: 51.5 us
  Pallas kernels  50.9 us (99%)
  between operations  0.64 us (1%)
    pallas_call x1, Pallas kernels, on_device(): pl.pallas_call(body, out_shape=(jax.ShapeDtypeStruct((256, F * D), F32),...  47.7 us
    pallas_call x1, Pallas kernels, on_device(): pl.pallas_call(finish, out_shape=(jax.ShapeDtypeStruct(((F - 1) * D, D),...  3.13 us

profile of v3, /device:TPU:1, one launch (start us, length us, event | category | flops | bytes accessed | tf_op | source)
XLA Modules:
  0.0 51.5 jit_solution(16819283741564600897)
XLA Ops:
  0.6 47.7 %shard_map.77 = (f32[256,1024]{1,0:T(8,128)}, bf16[32,32,128]{2,1,0:T(8,128)(2,1)}, s32[8,128]{1,0:T(8,128)}, bf16[14,2,32,128]{3,2,1,0:T(8,128)(2,1)}) custom-call(bf16[1024,128]{1,0:T(8,128)(2,1)} %bitcast.14, bf16[28,128,128]{2,1,0:T(8,128)(2,1)} %bitcast.13, bf16[7,128,128]{2,1,0:T(8,128)(2,1)} %bil_h.1, s32[8,4,128]{2,1,0:T(4,128)} %bitcast.16, ...), custom_call_target="tpu_custom_call" | custom-call | tf_op jit(solution)/shard_map/pallas_call | solution.py:538
  48.4 3.1 %shard_map.78 = (f32[896,128]{1,0:T(8,128)}, f32[2048,128]{1,0:T(8,128)}) custom-call(f32[256,1024]{1,0:T(8,128)} %get-tuple-element.8.acc_h, bf16[32,32,128]{2,1,0:T(8,128)(2,1)} %get-tuple-element.9.got_h, s32[8,128]{1,0:T(8,128)} %get-tuple-element.10.code_h, bf16[896,128]{1,0:T(8,128)(2,1)} %bitcast.15), custom_call_target="tpu_custom_call" | custom-call | tf_op jit(solution)/shard_map/pallas_call | solution.py:600

commit v4 on v3

--- a/solution.py
+++ b/solution.py
@@ -16,7 +16,7 @@
 NZ = 8
 NP = 32
 ROWS = F * TOK
-NCH = 2
+NCH = 4
 RED = 28
 PAIR = {(i, j): p for p, (i, j) in enumerate((i, j) for i in range(F) for j in range(i + 1, F))}
 F32, BF16, I32, I16 = jnp.float32, jnp.bfloat16, jnp.int32, jnp.int16
@@ -105,7 +105,7 @@
 ):
     gx, gy = lax.axis_index("gx"), lax.axis_index("gy")
     z, me = gx // 2, (gx % 2) * 16 + gy
-    up_z, dn_z = (z + 1) % NZ, (z + 7) % NZ
+    core = gy % 2
 
     loads = [
         pltpu.make_async_copy(a, b, lsem.at[n])
@@ -166,6 +166,46 @@
                 for k in range(0 if i < F - 1 else 1, i):
                     run = run + cot[PAIR[k, i], rows, :].astype(F32) * proj[k, rows, :]
                 vbuf[0, pl.ds(pl.multiple_of(i * 128 + r * 16, 16), 16), :] = run.astype(BF16)
+
+    with jax.named_scope("barrier"):
+        pl.semaphore_wait(bar, NP - 1 + NZ - 1)
+
+    piece = ROWS // NCH
+
+    def zcopy(e, t, c):
+        src = jnp.where(t == 1, 0, 2 * t - 3 + e)
+        dst = jnp.where(t == 4, 7, 2 * t - 1 + e)
+        at = jnp.where(e == 0, c, NCH - 1 - c)
+        rows = pl.ds(pl.multiple_of(at * piece, piece), piece)
+        to = (z + jnp.where(e == core, 1, NZ - 1)) % NZ
+        return pltpu.make_async_remote_copy(
+            vbuf.at[src, rows], vbuf.at[dst, rows], zs.at[e, t - 1, c], zr.at[e, t - 1, c],
+            device_id=dev(to, me), device_id_type=MESH,
+        )
+
+    def first_hop(e):
+        for c in range(NCH):
+            zcopy(e, 1, c).start()
+
+    first_hop(0)
+
+    def w2copy(r):
+        return pltpu.make_async_remote_copy(
+            share.at[pl.ds(pl.multiple_of(r * 32, 32), 32)], w2.at[me], ws.at[0], wr.at[0],
+            device_id=dev(z, r), device_id_type=MESH,
+        )
+
+    def shares_out():
+        @pl.loop(0, NP)
+        def _(j):
+            r = me ^ j
+
+            @pl.when((r < RED) & (j > 0))
+            def _():
+                w2copy(r).start()
+
+    with jax.named_scope("shares_out"):
+        shares_out()
 
     with jax.named_scope("lookup"):
         loads[3].wait()
@@ -186,43 +226,7 @@
                 loc[row : row + 1, :] = colsum(only(mask, out[128:, cols]))
                 live[row : row + 1, :] = jnp.where(lens[f : f + 1, :] > k, float(f + 1), 0.0)
 
-    with jax.named_scope("barrier"):
-        pl.semaphore_wait(bar, NP - 1 + NZ - 1)
-
-    half = ROWS // NCH
-
-    def zcopy(d, t, c):
-        src, dst = (t - 1, t) if d == 0 else ((8 - (t - 1)) % 8, 8 - t)
-        rows = pl.ds(c * half, half)
-        return pltpu.make_async_remote_copy(
-            vbuf.at[src, rows], vbuf.at[dst, rows], zs.at[d, t - 1, c], zr.at[d, t - 1, c],
-            device_id=dev(up_z if d == 0 else dn_z, me), device_id_type=MESH,
-        )
-
-    def first_hop(pieces):
-        for c in pieces:
-            for d in range(2):
-                zcopy(d, 1, c).start()
-
-    first_hop(range(NCH // 2))
-
-    def w2copy(r):
-        return pltpu.make_async_remote_copy(
-            share.at[pl.ds(pl.multiple_of(r * 32, 32), 32)], w2.at[me], ws.at[0], wr.at[0],
-            device_id=dev(z, r), device_id_type=MESH,
-        )
-
-    def shares_out():
-        @pl.loop(0, NP)
-        def _(j):
-            r = me ^ j
-
-            @pl.when((r < RED) & (j > 0))
-            def _():
-                w2copy(r).start()
-
-    with jax.named_scope("shares_out"):
-        shares_out()
+    first_hop(1)
 
     with jax.named_scope("rank"):
         tri = jnp.where(iota((256, 256), 0) < iota((256, 256), 1), 1.0, 0.0).astype(BF16)
@@ -253,17 +257,17 @@
         m4[...] = jnp.where(b1 > 0, (b1 - 1.0) + 128.0 * f1 + 2048.0 * table[:64, 128:], 0.0).astype(I32)
     mall[0] = m4[pl.ds(pl.multiple_of(z * 8, 8), 8), :]
 
-    def mcopy(t):
-        to = (z + t) % NZ
-        return pltpu.make_async_remote_copy(
-            m4.at[pl.ds(pl.multiple_of(to * 8, 8), 8)], mall.at[t], ms, mr.at[t], device_id=dev(to, me), device_id_type=MESH
+    def mcopy(n):
+        t = (n + 1) // 2
+        to = (z + jnp.where((n - 1) % 2 == core, t, NZ - t)) % NZ
+        return pltpu.make_async_remote_copy(
+            m4.at[pl.ds(pl.multiple_of(to * 8, 8), 8)], mall.at[n], ms, mr.at[n], device_id=dev(to, me), device_id_type=MESH
         )
 
     @pl.loop(1, NZ)
     def _(t):
         mcopy(t).start()
 
-    first_hop(range(NCH // 2, NCH))
 
     lane128 = iota((128, 128), 1).astype(I16)
 
@@ -282,13 +286,11 @@
 
     def send(idx):
         got[idx, me] = stage[idx, me]
-
-        @pl.loop(1, NP)
-        def _(j):
+        for j in range(1, NP):
             xycopy(idx, me ^ j).start()
 
     def last_own():
-        return pltpu.make_async_copy(stage.at[4, me], got_o.at[me], lsem.at[6])
+        return pltpu.make_async_copy(stage.at[7, me], got_o.at[me], lsem.at[6])
 
     def send_last():
         last_own().start()
@@ -296,7 +298,7 @@
         @pl.loop(1, NP)
         def _(j):
             pltpu.make_async_remote_copy(
-                stage.at[4, me ^ j], got_o.at[me], ss.at[4], rr.at[4], device_id=dev(z, me ^ j), device_id_type=MESH
+                stage.at[7, me ^ j], got_o.at[me], ss.at[7], rr.at[7], device_id=dev(z, me ^ j), device_id_type=MESH
             ).start()
 
     def accumulate(idx):
@@ -310,8 +312,8 @@
         )
 
     def targets_out():
-        for t in range(2, NZ - 1):
-            mcopy(t).wait_recv()
+        for n in range(3, NZ):
+            mcopy(n).wait_recv()
         mine = iota((8, 128), 1) // CAP == me % 4
         for pq in range(8):
             x = mall[:, pq, :] >> 7
@@ -404,49 +406,44 @@
 
         w4side().start()
 
-    def at(n):
-        return jnp.where(n == 7, 4, jnp.where(n % 2 == 1, (n + 1) // 2, (8 - n // 2) % 8))
-
     acc[...] = jnp.zeros_like(acc)
 
-    def pass_on(t, c):
-        for d in range(2):
-            with jax.named_scope("waitz"):
-                zcopy(d, t, c).wait_recv()
-
-            @pl.when((t < 3) | ((c < NCH // 2) == (d == 0)))
-            def _():
-                zcopy(d, t + 1, c).start()
+    def pass_on(n, c):
+        e, t = (n - 1) % 2, (n + 1) // 2
+        with jax.named_scope(f"waitz{c}"):
+            zcopy(e, t, c).wait_recv()
+
+        @pl.when((t < 3) | (c < NCH // 2))
+        def _():
+            zcopy(e, t + 1, c).start()
 
     @pl.loop(0, 9)
     def _(n):
-        t = (n + 1) // 2
-
-        @pl.when((n % 2 == 1) & (n < 7))
-        def _():
-            for c in range(NCH // 2, NCH):
-                pass_on(t, c)
+        @pl.when((n > 0) & (n < 7))
+        def _():
+            pass_on(n, 3)
 
         @pl.when(n == 7)
         def _():
-            for c in range(NCH // 2):
-                zcopy(0, 4, c).wait_recv()
-                zcopy(1, 4, c + NCH // 2).wait_recv()
+            with jax.named_scope("waitz4"):
+                for c in range(NCH // 2):
+                    for e in range(2):
+                        zcopy(e, 4, c).wait_recv()
 
         @pl.when(n < 8)
         def _():
             @pl.when((n == 1) | (n == 2))
             def _():
                 with jax.named_scope("waitm"):
-                    mcopy(at(n)).wait_recv()
+                    mcopy(n).wait_recv()
 
             with jax.named_scope("gather"):
-                gather(at(n))
+                gather(n)
 
             @pl.when(n < 7)
             def _():
                 with jax.named_scope("send"):
-                    send(at(n))
+                    send(n)
 
             @pl.when(n == 7)
             def _():
@@ -454,60 +451,46 @@
                     send_last()
 
 
-        @pl.when((n % 2 == 0) & (n < 6))
-        def _():
-            for c in range(NCH // 2):
-                pass_on(t + 1, c)
-
-        @pl.when(n == 2)
-        def _():
-            with jax.named_scope("targets_out"):
-                targets_out()
-
-        @pl.when(n == 1)
-        def _():
-            with jax.named_scope("weight_add"):
-                weight_add()
-
-        @pl.when(n == 3)
-        def _():
-            with jax.named_scope("weight_column"):
-                weight_column()
-
-        @pl.when(n == 4)
-        def _():
-            with jax.named_scope("targets_in"):
-                targets_in()
-
-        @pl.when(n == 5)
-        def _():
-            with jax.named_scope("weight_spread"):
-                weight_spread()
-
-        @pl.when(n == 8)
-        def _():
-            with jax.named_scope("weight_side"):
-                weight_side()
-
-        first = jnp.where(n <= 4, 0, jnp.where(n <= 6, n - 4, jnp.where(n == 7, 4, 5)))
-        last = jnp.where(n < 4, 0, jnp.where(n <= 5, n - 3, jnp.where(n == 6, 4, jnp.where(n == 7, 5, 7))))
-
-        @pl.loop(first, last)
-        def _(m):
-            with jax.named_scope("acc"):
-                accumulate(at(m))
-
-    w4side().wait()
-    outs = [
-        pltpu.make_async_copy(a, b, lsem.at[n])
-        for n, (a, b) in enumerate([(acc, acc_o), (cbuf.at[4], code_o), (w4, w4_o)])
-    ]
+        def once(when, what):
+            @pl.when(n == when)
+            def _():
+                with jax.named_scope(what.__name__):
+                    what()
+
+        def add(lo, hi):
+            @pl.loop(lo, hi)
+            def _(m):
+                with jax.named_scope("acc"):
+                    accumulate(m)
+
+        @pl.when(n < 6)
+        def _():
+            pass_on(n + 1, 0)
+            pass_on(n + 1, 1)
+
+        once(1, weight_add)
+        once(2, targets_out)
+        once(3, weight_column)
+        once(4, targets_in)
+        once(5, weight_spread)
+        once(8, weight_side)
+        add(jnp.where(n <= 4, 0, n - 4), jnp.where(n < 4, 0, jnp.where(n == 8, 7, n - 3)))
+
+        @pl.when(n < 6)
+        def _():
+            pass_on(n + 1, 2)
+
+    outs = [pltpu.make_async_copy(acc, acc_o, lsem.at[0]), pltpu.make_async_copy(cbuf.at[7], code_o, lsem.at[1])]
     for c in outs:
         c.start()
+    with jax.named_scope("waitside"):
+        w4side().wait()
+    outs.append(pltpu.make_async_copy(w4, w4_o, lsem.at[2]))
+    outs[-1].start()
     for t in range(1, 5):
         for d in range(2):
             for c in range(NCH):
-                if t < 4 or (c < NCH // 2) == (d == 0):
+                if t < 4 or c < NCH // 2:
                     zcopy(d, t, c).wait_send()
     wait_all(mall.at[pl.ds(0, NZ - 1)], ms)
     wait_all(dsend.at[pl.ds(0, NP - 1)], ds_)
@@ -529,7 +512,7 @@
         c.wait()
     last_own().wait()
     with jax.named_scope("waitxy"):
-        wait_all(got_o.at[pl.ds(0, NP - 1)], rr.at[4])
+        wait_all(got_o.at[pl.ds(0, NP - 1)], rr.at[7])
 
 
 def on_device(pooled, cotangent, bilinear, bag_ids, bag_lens, row_home):

time: 51.6 us -> 49.7 us (0.963)
  Pallas kernels: 50.9 us -> 49 us
    pallas_call x1, Pallas kernels: 47.7 us -> 45.9 us  [on_device(): pl.pallas_call(body, out_shape=(jax.ShapeDtypeStruct((256, F * D), F32),...]
where the time goes in v4:
time: 49.7 us; the launch traced here: 49.6 us
  Pallas kernels  49 us (99%)
  between operations  0.64 us (1%)
    pallas_call x1, Pallas kernels, on_device(): pl.pallas_call(body, out_shape=(jax.ShapeDtypeStruct((256, F * D), F32),...  45.9 us
    pallas_call x1, Pallas kernels, on_device(): pl.pallas_call(finish, out_shape=(jax.ShapeDtypeStruct(((F - 1) * D, D),...  3.13 us

profile of v4, /device:TPU:1, one launch (start us, length us, event | category | flops | bytes accessed | tf_op | source)
XLA Modules:
  0.0 49.6 jit_solution(3944003930370514559)
XLA Ops:
  0.6 45.9 %shard_map.77 = (f32[256,1024]{1,0:T(8,128)}, bf16[32,32,128]{2,1,0:T(8,128)(2,1)}, s32[8,128]{1,0:T(8,128)}, bf16[14,2,32,128]{3,2,1,0:T(8,128)(2,1)}) custom-call(bf16[1024,128]{1,0:T(8,128)(2,1)} %bitcast.14, bf16[28,128,128]{2,1,0:T(8,128)(2,1)} %bitcast.13, bf16[7,128,128]{2,1,0:T(8,128)(2,1)} %bil_h.1, s32[8,4,128]{2,1,0:T(4,128)} %bitcast.16, ...), custom_call_target="tpu_custom_call" | custom-call | tf_op jit(solution)/shard_map/pallas_call | solution.py:521
  46.5 3.1 %shard_map.78 = (f32[896,128]{1,0:T(8,128)}, f32[2048,128]{1,0:T(8,128)}) custom-call(f32[256,1024]{1,0:T(8,128)} %get-tuple-element.8.acc_h, bf16[32,32,128]{2,1,0:T(8,128)(2,1)} %get-tuple-element.9.got_h, s32[8,128]{1,0:T(8,128)} %get-tuple-element.10.code_h, bf16[896,128]{1,0:T(8,128)(2,1)} %bitcast.15), custom_call_target="tpu_custom_call" | custom-call | tf_op jit(solution)/shard_map/pallas_call | solution.py:583

commit v5 on v4

--- a/solution.py
+++ b/solution.py
@@ -118,13 +118,10 @@
 
     bar = pltpu.get_barrier_semaphore()
 
-    @pl.loop(1, NP)
-    def _(j):
+    for t in (4, 3, 5, 2, 6, 1, 7):
+        pl.semaphore_signal(bar, inc=1, device_id=dev((z + t) % NZ, me), device_id_type=MESH)
+    for j in range(NP - 1, 0, -1):
         pl.semaphore_signal(bar, inc=1, device_id=dev(z, me ^ j), device_id_type=MESH)
-
-    @pl.loop(1, NZ)
-    def _(t):
-        pl.semaphore_signal(bar, inc=1, device_id=dev((z + t) % NZ, me), device_id_type=MESH)
 
     with jax.named_scope("perm"):
         loads[0].wait()
@@ -134,38 +131,30 @@
         for g in range(8):
             for f in range(F):
                 pf[f, pl.ds(g * 16, 16), :] = y[f * 16 : f * 16 + 16, g * 128 : g * 128 + 128]
-    with jax.named_scope("proj"):
+    with jax.named_scope("grads"):
         loads[1].wait()
+        loads[2].wait()
         for i in range(F - 1):
             proj[i] = dot(pf[i], bil[i])
-        loads[2].wait()
-
-    with jax.named_scope("upper"):
-        @pl.loop(0, 8)
-        def _(r):
-            rows = pl.ds(pl.multiple_of(r * 16, 16), 16)
+        for r in range(0, TOK, 16):
+            rows = pl.ds(r, 16)
             pj = [pf[j, rows, :].astype(F32) for j in range(F)]
             for i in range(F - 1):
                 run = cot[PAIR[i, i + 1], rows, :].astype(F32) * pj[i + 1]
                 for j in range(i + 2, F):
                     run = run + cot[PAIR[i, j], rows, :].astype(F32) * pj[j]
                 up[i, rows, :] = run.astype(BF16)
-
-    with jax.named_scope("mm"):
         for i in range(F - 1):
             back[i] = dot(up[i], bil[i], 1, 1)
-        for i in range(F - 1):
-            share[pl.ds(i * 128, 128), :] = dot(pf[i], up[i], 0, 0).astype(BF16)
-
-    with jax.named_scope("fgrad"):
-        @pl.loop(0, 8)
-        def _(r):
-            rows = pl.ds(pl.multiple_of(r * 16, 16), 16)
+        for r in range(0, TOK, 16):
+            rows = pl.ds(r, 16)
             for i in range(F):
                 run = back[i, rows, :] if i < F - 1 else cot[PAIR[0, i], rows, :].astype(F32) * proj[0, rows, :]
                 for k in range(0 if i < F - 1 else 1, i):
                     run = run + cot[PAIR[k, i], rows, :].astype(F32) * proj[k, rows, :]
-                vbuf[0, pl.ds(pl.multiple_of(i * 128 + r * 16, 16), 16), :] = run.astype(BF16)
+                vbuf[0, pl.ds(i * TOK + r, 16), :] = run.astype(BF16)
+        for i in range(F - 1):
+            share[pl.ds(i * D, D), :] = dot(pf[i], up[i], 0, 0).astype(BF16)
 
     with jax.named_scope("barrier"):
         pl.semaphore_wait(bar, NP - 1 + NZ - 1)
@@ -207,54 +196,55 @@
     with jax.named_scope("shares_out"):
         shares_out()
 
-    with jax.named_scope("lookup"):
-        loads[3].wait()
-        loads[4].wait()
-        loads[5].wait()
-        hi_iota, lo_iota = iota((512, 128), 0).astype(I16), bf(iota((128, 128), 0))
-        for f in range(F):
-            t = home[pl.ds(f, 512, stride=F), :].T
-            table = bf(jnp.concatenate([t >> 8, t & 255], axis=0))
-            hi, lo = (ids[f] >> 7).astype(I16), bf(ids[f] & 127)
-            oh = jnp.concatenate([onehot(hi_iota == hi[k : k + 1]) for k in range(BAG)], axis=1)
-            out = dot(table, oh).astype(BF16)
-            for k in range(BAG):
-                mask = lo_iota == lo[k : k + 1]
-                cols = slice(k * 128, k * 128 + 128)
-                row = f * BAG + k
-                own[row : row + 1, :] = colsum(only(mask, out[:128, cols])).astype(I32)
-                loc[row : row + 1, :] = colsum(only(mask, out[128:, cols]))
-                live[row : row + 1, :] = jnp.where(lens[f : f + 1, :] > k, float(f + 1), 0.0)
+    @pl.when(gx >= 0)
+    def _():
+        with jax.named_scope("lookup"):
+            loads[3].wait()
+            loads[4].wait()
+            loads[5].wait()
+            hi_iota, lo_iota = iota((512, 128), 0).astype(I16), bf(iota((128, 128), 0))
+            for f in range(F):
+                t = home[pl.ds(f, 512, stride=F), :].T
+                table = bf(jnp.concatenate([t >> 8, t & 255], axis=0))
+                hi, lo = (ids[f] >> 7).astype(I16), bf(ids[f] & 127)
+                oh = jnp.concatenate([onehot(hi_iota == hi[k : k + 1]) for k in range(BAG)], axis=1)
+                out = dot(table, oh).astype(BF16)
+                for k in range(BAG):
+                    mask = lo_iota == lo[k : k + 1]
+                    cols = slice(k * 128, k * 128 + 128)
+                    row = f * BAG + k
+                    own[row : row + 1, :] = colsum(only(mask, out[:128, cols])).astype(I32)
+                    loc[row : row + 1, :] = colsum(only(mask, out[128:, cols]))
+                    live[row : row + 1, :] = jnp.where(lens[f : f + 1, :] > k, float(f + 1), 0.0)
 
     first_hop(1)
 
-    with jax.named_scope("rank"):
-        tri = jnp.where(iota((256, 256), 0) < iota((256, 256), 1), 1.0, 0.0).astype(BF16)
-        tri = jnp.concatenate([tri, jnp.ones((256, 128), BF16)], axis=1)
-        own_iota, o4_iota, rr_iota = bf(iota((256, 128), 0)), bf(iota((64, 128), 0)), bf(iota((128, 128), 0))
-        lane = bf(iota((1, 128), 1) + 1)
-        o = own[...]
-        o_b, o4_b, oc_b = bf(o), bf(o >> 2), bf((o & 3) * CAP)
-        loc_b, live_b = loc[...].astype(BF16), live[...].astype(BF16)
-        before = jnp.zeros((256, 128), BF16)
-        table, lhs, rhs = jnp.zeros((128, 256), F32), [], []
-        for j in range(16):
-            hit = [own_iota == o_b[r : r + 1] for r in (2 * j, 2 * j + 1)]
-            res = dot(jnp.concatenate([onehot(h) for h in hit], axis=1), tri).astype(BF16)
-            for n in range(2):
-                r = slice(2 * j + n, 2 * j + n + 1)
-                rank = colsum(only(hit[n], res[:, n * 128 : n * 128 + 128] + before))
-                spot = rr_iota == oc_b[r] + rank.astype(BF16)
-                four = o4_iota == o4_b[r]
-                rhs.append(jnp.concatenate([only(spot, lane), only(spot, loc_b[r])], axis=0))
-                lhs.append(jnp.concatenate([onehot(four), only(four, live_b[r])], axis=0))
-            before = before + res[:, 256:]
-            if j % 4 == 3:
-                table = table + dot(jnp.concatenate(lhs, axis=1), jnp.concatenate(rhs, axis=1), 1, 1)
-                lhs, rhs = [], []
-        b1 = table[:64, :128]
-        f1 = jnp.round(table[64:, :128] / jnp.maximum(b1, 1.0))
-        m4[...] = jnp.where(b1 > 0, (b1 - 1.0) + 128.0 * f1 + 2048.0 * table[:64, 128:], 0.0).astype(I32)
+    @pl.when(gx >= 0)
+    def _():
+        with jax.named_scope("rank"):
+            tri = jnp.where(iota((256, 256), 0) <= iota((256, 256), 1), 1.0, 0.0).astype(BF16)
+            own_iota, o4_iota, rr_iota = bf(iota((256, 128), 0)), bf(iota((64, 128), 0)), bf(iota((128, 128), 0))
+            lane = bf(iota((1, 128), 1) + 1)
+            o = own[...]
+            o_b, o4_b, oc_b = bf(o), bf(o >> 2), bf((o & 3) * CAP - 1)
+            loc_b, live_b = loc[...].astype(BF16), live[...].astype(BF16)
+            before = jnp.zeros((256, 128), BF16)
+            lhs, rhs = [], []
+            for j in range(16):
+                hit = [own_iota == o_b[r : r + 1] for r in (2 * j, 2 * j + 1)]
+                count = dot(jnp.concatenate([onehot(h) for h in hit], axis=1), tri).astype(BF16)
+                for n in range(2):
+                    r = slice(2 * j + n, 2 * j + n + 1)
+                    rank = colsum(only(hit[n], count[:, n * 128 : n * 128 + 128] + before))
+                    spot = rr_iota == oc_b[r] + rank.astype(BF16)
+                    four = o4_iota == o4_b[r]
+                    lhs.append(jnp.concatenate([only(spot, lane), only(spot, loc_b[r])], axis=0))
+                    rhs.append(jnp.concatenate([onehot(four), only(four, live_b[r])], axis=0))
+                before = before + jnp.broadcast_to(count[:, 255:], (256, 128))
+            table = dot(jnp.concatenate(lhs, axis=1), jnp.concatenate(rhs, axis=1), 1, 1).T
+            b1 = table[:64, :128]
+            f1 = jnp.round(table[64:, :128] / jnp.maximum(b1, 1.0))
+            m4[...] = jnp.where(b1 > 0, (b1 - 1.0) + 128.0 * f1 + 2048.0 * table[:64, 128:], 0.0).astype(I32)
     mall[0] = m4[pl.ds(pl.multiple_of(z * 8, 8), 8), :]
 
     def mcopy(n):
@@ -294,9 +284,7 @@
 
     def send_last():
         last_own().start()
-
-        @pl.loop(1, NP)
-        def _(j):
+        for j in range(1, NP):
             pltpu.make_async_remote_copy(
                 stage.at[7, me ^ j], got_o.at[me], ss.at[7], rr.at[7], device_id=dev(z, me ^ j), device_id_type=MESH
             ).start()
@@ -306,6 +294,10 @@
             wait_all(got.at[idx, pl.ds(0, NP - 1)], rr.at[idx])
         add_slots(cbuf[idx], got.at[idx], acc)
 
+    def fold(y):
+        y = y + pltpu.roll(y, 7, 0)
+        return y + pltpu.roll(y, 6, 0)
+
     def dcopy(q):
         return pltpu.make_async_remote_copy(
             dsend.at[q], drecv.at[me], ds_, dr, device_id=dev(z, q), device_id_type=MESH
@@ -314,12 +306,14 @@
     def targets_out():
         for n in range(3, NZ):
             mcopy(n).wait_recv()
-        mine = iota((8, 128), 1) // CAP == me % 4
+        row4, block = iota((8, 128), 0) % 4, iota((8, 128), 1) // CAP
         for pq in range(8):
             x = mall[:, pq, :] >> 7
-            for s in range(4):
-                y = pltpu.roll(x, s * CAP, 1) if s else x
-                dsend[pq * 4 + (me % 4 + 4 - s) % 4] = jnp.where(mine, y, 0).astype(I16)
+            turned = [pltpu.roll(x, s * CAP, 1) if s else x for s in range(4)]
+            for j in range(4):
+                y = sum(jnp.where((block == row4) & ((row4 + 4 - j) % 4 == s), turned[s], 0) for s in range(4))
+                y = fold(y)
+                dsend[pq * 4 + j] = y[0:1] + (y[4:5] << 16)
         drecv[me] = dsend[me]
 
         @pl.loop(1, NP)
@@ -329,8 +323,17 @@
     def targets_in():
         many = drecv.at[pl.ds(0, NP - 1)]
         pltpu.make_async_copy(many, many, dr).wait()
-        for g in range(8):
-            cbuf[:, g, :] = sum(drecv[4 * g + n].astype(I32) for n in range(4))
+        row4, block = iota((8, 128), 0) % 4, iota((8, 128), 1) // CAP
+        for v in range(4):
+            words = drecv[pl.ds(v * 8, 8)].reshape(8, 128)
+            for r in range(2):
+                x = (words >> 16) if r else (words & 0xFFFF)
+                turned = [pltpu.roll(x, s * CAP, 1) if s else x for s in range(4)]
+                for m in range(4):
+                    y = sum(jnp.where((block == row4) & ((row4 + 4 - m) % 4 == s), turned[s], 0) for s in range(4))
+                    y = fold(y)
+                    for h in range(2):
+                        cbuf[4 * r + m, 2 * v + h : 2 * v + h + 1, :] = y[4 * h : 4 * h + 1]
 
     def w3copy(t):
         to = (z + t) % NZ
@@ -421,6 +424,12 @@
     def _(n):
         @pl.when((n > 0) & (n < 7))
         def _():
+            pass_on(n, 2)
+
+            @pl.when(n < 6)
+            def _():
+                pass_on(n + 1, 0)
+
             pass_on(n, 3)
 
         @pl.when(n == 7)
@@ -463,22 +472,22 @@
                 with jax.named_scope("acc"):
                     accumulate(m)
 
+        @pl.when(n == 0)
+        def _():
+            pass_on(1, 0)
+
         @pl.when(n < 6)
         def _():
-            pass_on(n + 1, 0)
             pass_on(n + 1, 1)
 
         once(1, weight_add)
         once(2, targets_out)
         once(3, weight_column)
-        once(4, targets_in)
+        once(5, targets_in)
         once(5, weight_spread)
+        add(jnp.where(n <= 5, 0, 1), jnp.where(n < 5, 0, jnp.where(n == 8, 6, 1)))
         once(8, weight_side)
-        add(jnp.where(n <= 4, 0, n - 4), jnp.where(n < 4, 0, jnp.where(n == 8, 7, n - 3)))
-
-        @pl.when(n < 6)
-        def _():
-            pass_on(n + 1, 2)
+        add(6, jnp.where(n == 8, 7, 6))
 
     outs = [pltpu.make_async_copy(acc, acc_o, lsem.at[0]), pltpu.make_async_copy(cbuf.at[7], code_o, lsem.at[1])]
     for c in outs:
@@ -545,8 +554,8 @@
             pltpu.VMEM((F * BAG, 128), F32),
             pltpu.VMEM((64, 128), I32),
             pltpu.VMEM((NZ, 8, 128), I32),
-            pltpu.VMEM((NP, 8, 128), I16),
-            pltpu.VMEM((NP, 8, 128), I16),
+            pltpu.VMEM((NP, 1, 128), I32),
+            pltpu.VMEM((NP, 1, 128), I32),
             pltpu.VMEM((NZ, 8, 128), I32),
             pltpu.VMEM((NZ, ROWS, D), BF16),
             pltpu.VMEM((NZ, NP, CAP, D), BF16),

time: 49.7 us -> 49.1 us (0.988)
  Pallas kernels: 49 us -> 48.4 us
    pallas_call x1, Pallas kernels: 45.9 us -> 45.3 us  [on_device(): pl.pallas_call(body, out_shape=(jax.ShapeDtypeStruct((256, F * D), F32),...]
where the time goes in v5:
time: 49.1 us; the launch traced here: 49 us
  Pallas kernels  48.4 us (99%)
  between operations  0.64 us (1%)
    pallas_call x1, Pallas kernels, on_device(): pl.pallas_call(body, out_shape=(jax.ShapeDtypeStruct((256, F * D), F32),...  45.3 us
    pallas_call x1, Pallas kernels, on_device(): pl.pallas_call(finish, out_shape=(jax.ShapeDtypeStruct(((F - 1) * D, D),...  3.13 us

profile of v5, /device:TPU:1, one launch (start us, length us, event | category | flops | bytes accessed | tf_op | source)
XLA Modules:
  0.0 49.0 jit_solution(13909391873095551923)
XLA Ops:
  0.6 45.3 %shard_map.77 = (f32[256,1024]{1,0:T(8,128)}, bf16[32,32,128]{2,1,0:T(8,128)(2,1)}, s32[8,128]{1,0:T(8,128)}, bf16[14,2,32,128]{3,2,1,0:T(8,128)(2,1)}) custom-call(bf16[1024,128]{1,0:T(8,128)(2,1)} %bitcast.14, bf16[28,128,128]{2,1,0:T(8,128)(2,1)} %bitcast.13, bf16[7,128,128]{2,1,0:T(8,128)(2,1)} %bil_h.1, s32[8,4,128]{2,1,0:T(4,128)} %bitcast.16, ...), custom_call_target="tpu_custom_call" | custom-call | tf_op jit(solution)/shard_map/pallas_call | solution.py:530
  45.9 3.1 %shard_map.78 = (f32[896,128]{1,0:T(8,128)}, f32[2048,128]{1,0:T(8,128)}) custom-call(f32[256,1024]{1,0:T(8,128)} %get-tuple-element.8.acc_h, bf16[32,32,128]{2,1,0:T(8,128)(2,1)} %get-tuple-element.9.got_h, s32[8,128]{1,0:T(8,128)} %get-tuple-element.10.code_h, bf16[896,128]{1,0:T(8,128)(2,1)} %bitcast.15), custom_call_target="tpu_custom_call" | custom-call | tf_op jit(solution)/shard_map/pallas_call | solution.py:592

commit v6 on v5

--- a/solution.py
+++ b/solution.py
@@ -19,6 +19,7 @@
 NCH = 4
 RED = 28
 PAIR = {(i, j): p for p, (i, j) in enumerate((i, j) for i in range(F) for j in range(i + 1, F))}
+STEPS = ((2, 2), (1, 2), (2, 1), (3, 2), (2, 3), (1, 1), (3, 3), (2, 0), (0, 2), (1, 3), (3, 1), (1, 0), (0, 1), (3, 0), (0, 3))
 F32, BF16, I32, I16 = jnp.float32, jnp.bfloat16, jnp.int32, jnp.int16
 
 
@@ -80,7 +81,7 @@
     loads[1].wait()
     add_slots(code[...], got, part)
     loads[2].wait()
-    wg[...] = w4[...].astype(F32)
+    wg[...] = w4[...].astype(F32).reshape((F - 1) * D, D)
     wg_out = pltpu.make_async_copy(wg, wg_o, sem.at[4])
     wg_out.start()
     loads[3].wait()
@@ -100,7 +101,7 @@
     pf, up, proj, back, share,
     own, loc, live, m4, mall, dsend, drecv, cbuf,
     vbuf, stage, got,
-    acc, w2, w3, w4, part, done,
+    acc, w2, w3, w4, part,
     lsem, zs, zr, ms, mr, ds_, dr, ss, rr, ws, wr,
 ):
     gx, gy = lax.axis_index("gx"), lax.axis_index("gy")
@@ -274,19 +275,28 @@
             stage.at[idx, q], got.at[idx, me], ss.at[idx], rr.at[idx], device_id=dev(z, q), device_id_type=MESH
         )
 
+    way = 1 + 2 * core
+    at_x, at_y = (me // 2 % 2) * 2 + me // 16, me // 4 % 4
+
+    def chip(dx, dy, c):
+        x, y = (at_x + way * dx) % 4, (at_y + way * dy) % 4
+        return (x % 2) * 16 + y * 4 + (x // 2) * 2 + c
+
+    others = [chip(dx, dy, c) for dx, dy in STEPS for c in range(2)] + [me ^ 1]
+
     def send(idx):
         got[idx, me] = stage[idx, me]
-        for j in range(1, NP):
-            xycopy(idx, me ^ j).start()
+        for q in others:
+            xycopy(idx, q).start()
 
     def last_own():
         return pltpu.make_async_copy(stage.at[7, me], got_o.at[me], lsem.at[6])
 
     def send_last():
         last_own().start()
-        for j in range(1, NP):
+        for q in others:
             pltpu.make_async_remote_copy(
-                stage.at[7, me ^ j], got_o.at[me], ss.at[7], rr.at[7], device_id=dev(z, me ^ j), device_id_type=MESH
+                stage.at[7, q], got_o.at[me], ss.at[7], rr.at[7], device_id=dev(z, q), device_id_type=MESH
             ).start()
 
     def accumulate(idx):
@@ -303,17 +313,23 @@
             dsend.at[q], drecv.at[me], ds_, dr, device_id=dev(z, q), device_id_type=MESH
         )
 
-    def targets_out():
-        for n in range(3, NZ):
-            mcopy(n).wait_recv()
+    def targets_out(quads):
         row4, block = iota((8, 128), 0) % 4, iota((8, 128), 1) // CAP
-        for pq in range(8):
+        for pq in quads:
             x = mall[:, pq, :] >> 7
             turned = [pltpu.roll(x, s * CAP, 1) if s else x for s in range(4)]
             for j in range(4):
                 y = sum(jnp.where((block == row4) & ((row4 + 4 - j) % 4 == s), turned[s], 0) for s in range(4))
                 y = fold(y)
                 dsend[pq * 4 + j] = y[0:1] + (y[4:5] << 16)
+
+    def targets_first():
+        for n in range(3, NZ):
+            mcopy(n).wait_recv()
+        targets_out(range(4))
+
+    def targets_rest():
+        targets_out(range(4, 8))
         drecv[me] = dsend[me]
 
         @pl.loop(1, NP)
@@ -341,22 +357,25 @@
             part.at[to], w3.at[z], ws.at[1], wr.at[1], device_id=dev(to, me), device_id_type=MESH
         )
 
-    def w3back(t):
-        return pltpu.make_async_remote_copy(
-            done.at[z], done.at[z], ws.at[2], wr.at[2], device_id=dev((z + t) % NZ, me), device_id_type=MESH
-        )
-
-    def w4copy(q):
-        mine = w4.at[me // 2, me % 2]
-        return pltpu.make_async_remote_copy(
-            mine, mine, ws.at[3], wr.at[3], device_id=dev(z, q), device_id_type=MESH
+    def rows_copy(q):
+        mine = w4.at[me // 2, core, z]
+        return pltpu.make_async_remote_copy(
+            mine, mine, ws.at[2], wr.at[2], device_id=dev(z, q), device_id_type=MESH
+        )
+
+    def column_copy(t):
+        mine = w4.at[:, core, z]
+        return pltpu.make_async_remote_copy(
+            mine, mine, ws.at[3], wr.at[3], device_id=dev((z + t) % NZ, me), device_id_type=MESH
         )
 
     def w4side():
-        mine = w4.at[:, me % 2]
-        return pltpu.make_async_remote_copy(
-            mine, mine, ws.at[4], wr.at[4], device_id=dev(z, me ^ 1), device_id_type=MESH
-        )
+        return pltpu.make_async_remote_copy(
+            w4.at[:, core], w4_o.at[:, core], ws.at[4], wr.at[4], device_id=dev(z, me ^ 1), device_id_type=MESH
+        )
+
+    def w4own():
+        return pltpu.make_async_copy(w4.at[:, core], w4_o.at[:, core], lsem.at[2])
 
     adder = me < RED
 
@@ -382,32 +401,29 @@
             total = w3[0]
             for i in range(1, NZ):
                 total = total + w3[i]
-            done[z] = total
-
-            @pl.loop(1, NZ)
-            def _(t):
-                w3back(t).start()
+            w4[me // 2, core, z] = total.astype(BF16)
+
+            @pl.loop(1, NP // 2)
+            def _(j):
+                rows_copy(me ^ (2 * j)).start()
 
     def weight_spread():
         @pl.when(adder)
         def _():
-            wait_all(done.at[pl.ds(0, NZ - 1)], wr.at[2])
-            w4[me // 2, me % 2] = done[...].reshape(32, D).astype(BF16)
-
-            @pl.loop(1, NP // 2)
-            def _(j):
-                w4copy(me ^ (2 * j)).start()
+            wait_all(w4.at[pl.ds(0, RED // 2 - 1), 0, 0], wr.at[2])
+
+        @pl.when(me >= RED)
+        def _():
+            wait_all(w4.at[:, 0, 0], wr.at[2])
+
+        @pl.loop(1, NZ)
+        def _(t):
+            column_copy(t).start()
 
     def weight_side():
-        @pl.when(adder)
-        def _():
-            wait_all(w4.at[pl.ds(0, RED // 2 - 1), 0], wr.at[3])
-
-        @pl.when(me >= RED)
-        def _():
-            wait_all(w4.at[:, 0], wr.at[3])
-
+        wait_all(w4.at[:, 0, pl.ds(0, NZ - 1)], wr.at[3])
         w4side().start()
+        w4own().start()
 
     acc[...] = jnp.zeros_like(acc)
 
@@ -426,7 +442,7 @@
         def _():
             pass_on(n, 2)
 
-            @pl.when(n < 6)
+            @pl.when((n > 1) & (n < 6))
             def _():
                 pass_on(n + 1, 0)
 
@@ -472,30 +488,26 @@
                 with jax.named_scope("acc"):
                     accumulate(m)
 
-        @pl.when(n == 0)
-        def _():
-            pass_on(1, 0)
+        @pl.when(n < 2)
+        def _():
+            pass_on(n + 1, 0)
 
         @pl.when(n < 6)
         def _():
             pass_on(n + 1, 1)
 
         once(1, weight_add)
-        once(2, targets_out)
-        once(3, weight_column)
-        once(5, targets_in)
-        once(5, weight_spread)
-        add(jnp.where(n <= 5, 0, 1), jnp.where(n < 5, 0, jnp.where(n == 8, 6, 1)))
+        once(2, targets_first)
+        once(3, targets_rest)
+        once(4, weight_column)
+        once(6, targets_in)
+        once(7, weight_spread)
+        add(jnp.where(n == 8, 1, 0), jnp.where(n == 8, 7, jnp.where(n == 6, 1, 0)))
         once(8, weight_side)
-        add(6, jnp.where(n == 8, 7, 6))
 
     outs = [pltpu.make_async_copy(acc, acc_o, lsem.at[0]), pltpu.make_async_copy(cbuf.at[7], code_o, lsem.at[1])]
     for c in outs:
         c.start()
-    with jax.named_scope("waitside"):
-        w4side().wait()
-    outs.append(pltpu.make_async_copy(w4, w4_o, lsem.at[2]))
-    outs[-1].start()
     for t in range(1, 5):
         for d in range(2):
             for c in range(NCH):
@@ -503,6 +515,7 @@
                     zcopy(d, t, c).wait_send()
     wait_all(mall.at[pl.ds(0, NZ - 1)], ms)
     wait_all(dsend.at[pl.ds(0, NP - 1)], ds_)
+    wait_all(w4.at[:, 0, pl.ds(0, NZ - 1)], ws.at[3])
     for k in range(8):
         wait_all(stage.at[k, pl.ds(0, NP - 1)], ss.at[k])
 
@@ -510,8 +523,7 @@
     def _():
         wait_all(w2.at[pl.ds(0, RED - 1)], ws.at[0])
         wait_all(w3.at[pl.ds(0, NZ - 1)], ws.at[1])
-        wait_all(done.at[pl.ds(0, NZ - 1)], ws.at[2])
-        wait_all(w2.at[pl.ds(0, NP // 2 - 1)], ws.at[3])
+        wait_all(w4.at[pl.ds(0, 5), 0, pl.ds(0, 3)], ws.at[2])
 
     @pl.when(me >= RED)
     def _():
@@ -520,6 +532,9 @@
     for c in outs:
         c.wait()
     last_own().wait()
+    with jax.named_scope("waitside"):
+        w4own().wait()
+        w4side().wait()
     with jax.named_scope("waitxy"):
         wait_all(got_o.at[pl.ds(0, NP - 1)], rr.at[7])
 
@@ -533,7 +548,7 @@
             jax.ShapeDtypeStruct((256, F * D), F32),
             jax.ShapeDtypeStruct((NP, CAP, D), BF16),
             jax.ShapeDtypeStruct((8, 128), I32),
-            jax.ShapeDtypeStruct((RED // 2, 2, 32, D), BF16),
+            jax.ShapeDtypeStruct((RED // 2, 2, NZ, 4, D), BF16),
         ),
         in_specs=[any_] * 6,
         out_specs=[any_] * 4,
@@ -563,8 +578,7 @@
             pltpu.VMEM((256, F * D), F32),
             pltpu.VMEM((NP, 32, D), BF16),
             pltpu.VMEM((NZ, 4, D), F32),
-            pltpu.VMEM((RED // 2, 2, 32, D), BF16),
-            pltpu.VMEM((NZ, 4, D), F32),
+            pltpu.VMEM((RED // 2, 2, NZ, 4, D), BF16),
             pltpu.VMEM((NZ, 4, D), F32),
             dma((7,)),
             dma((2, 4, NCH)),
@@ -601,14 +615,14 @@
             pltpu.VMEM((256, F * D), F32),
             pltpu.VMEM((NP, CAP, D), BF16),
             pltpu.VMEM((8, 128), I32),
-            pltpu.VMEM(((F - 1) * D, D), BF16),
+            pltpu.VMEM(((F - 1) * D // 4, 4, D), BF16),
             pltpu.VMEM(((F - 1) * D, D), F32),
             pltpu.VMEM((256, F * D), F32),
             pltpu.VMEM((256 * F, D), F32),
             dma((6,)),
         ],
         compiler_params=pltpu.CompilerParams(vmem_limit_bytes=60 * 2**20),
-    )(acc, got, code, w4.reshape((F - 1) * D, D))
+    )(acc, got, code, w4.reshape((F - 1) * D // 4, 4, D))
     return wg.reshape(F - 1, D, D), table.reshape(256, F, D)
 
 

time: 49.1 us -> 48.2 us (0.982)
  Pallas kernels: 48.4 us -> 47.5 us
    pallas_call x1, Pallas kernels: 45.3 us -> 44.3 us  [on_device(): pl.pallas_call(body, out_shape=(jax.ShapeDtypeStruct((256, F * D), F32),...]
where the time goes in v6:
time: 48.2 us; the launch traced here: 48.1 us
  Pallas kernels  47.5 us (99%)
  between operations  0.64 us (1%)
    pallas_call x1, Pallas kernels, on_device(): pl.pallas_call(body, out_shape=(jax.ShapeDtypeStruct((256, F * D), F32),...  44.3 us
    pallas_call x1, Pallas kernels, on_device(): pl.pallas_call(finish, out_shape=(jax.ShapeDtypeStruct(((F - 1) * D, D),...  3.15 us

profile of v6, /device:TPU:1, one launch (start us, length us, event | category | flops | bytes accessed | tf_op | source)
XLA Modules:
  0.0 48.1 jit_solution(6559844737626236119)
XLA Ops:
  0.6 44.3 %shard_map.77 = (f32[256,1024]{1,0:T(8,128)}, bf16[32,32,128]{2,1,0:T(8,128)(2,1)}, s32[8,128]{1,0:T(8,128)}, bf16[14,2,8,4,128]{4,3,2,1,0:T(4,128)(2,1)}) custom-call(bf16[1024,128]{1,0:T(8,128)(2,1)} %bitcast.14, bf16[28,128,128]{2,1,0:T(8,128)(2,1)} %bitcast.13, bf16[7,128,128]{2,1,0:T(8,128)(2,1)} %bil_h.1, s32[8,4,128]{2,1,0:T(4,128)} %bitcast.16, ...), custom_call_target="tpu_custom_call" | custom-call | tf_op jit(solution)/shard_map/pallas_call | solution.py:545
  44.9 3.2 %shard_map.78 = (f32[896,128]{1,0:T(8,128)}, f32[2048,128]{1,0:T(8,128)}) custom-call(f32[256,1024]{1,0:T(8,128)} %get-tuple-element.8.acc_h, bf16[32,32,128]{2,1,0:T(8,128)(2,1)} %get-tuple-element.9.got_h, s32[8,128]{1,0:T(8,128)} %get-tuple-element.10.code_h, bf16[224,4,128]{2,1,0:T(4,128)(2,1)} %bitcast.15), custom_call_target="tpu_custom_call" | custom-call | tf_op jit(solution)/shard_map/pallas_call | solution.py:606

commit v7 on v6

--- a/solution.py
+++ b/solution.py
@@ -186,11 +186,10 @@
         )
 
     def shares_out():
-        @pl.loop(0, NP)
-        def _(j):
+        for j in range(1, NP):
             r = me ^ j
 
-            @pl.when((r < RED) & (j > 0))
+            @pl.when(r < RED)
             def _():
                 w2copy(r).start()
 
@@ -503,11 +502,12 @@
         once(6, targets_in)
         once(7, weight_spread)
         add(jnp.where(n == 8, 1, 0), jnp.where(n == 8, 7, jnp.where(n == 6, 1, 0)))
-        once(8, weight_side)
 
     outs = [pltpu.make_async_copy(acc, acc_o, lsem.at[0]), pltpu.make_async_copy(cbuf.at[7], code_o, lsem.at[1])]
     for c in outs:
         c.start()
+    with jax.named_scope("weight_side"):
+        weight_side()
     for t in range(1, 5):
         for d in range(2):
             for c in range(NCH):

time: 48.2 us -> 48.1 us (level)
  no operation moved by 1% of the time
where the time goes in v7:
time: 48.1 us; the launch traced here: 48 us
  Pallas kernels  47.3 us (98%)
  between operations  0.64 us (1%)
    pallas_call x1, Pallas kernels, on_device(): pl.pallas_call(body, out_shape=(jax.ShapeDtypeStruct((256, F * D), F32),...  44.2 us
    pallas_call x1, Pallas kernels, on_device(): pl.pallas_call(finish, out_shape=(jax.ShapeDtypeStruct(((F - 1) * D, D),...  3.15 us

profile of v7, /device:TPU:1, one launch (start us, length us, event | category | flops | bytes accessed | tf_op | source)
XLA Modules:
  0.0 48.0 jit_solution(9220583132598645640)
XLA Ops:
  0.6 44.2 %shard_map.77 = (f32[256,1024]{1,0:T(8,128)}, bf16[32,32,128]{2,1,0:T(8,128)(2,1)}, s32[8,128]{1,0:T(8,128)}, bf16[14,2,8,4,128]{4,3,2,1,0:T(4,128)(2,1)}) custom-call(bf16[1024,128]{1,0:T(8,128)(2,1)} %bitcast.14, bf16[28,128,128]{2,1,0:T(8,128)(2,1)} %bitcast.13, bf16[7,128,128]{2,1,0:T(8,128)(2,1)} %bil_h.1, s32[8,4,128]{2,1,0:T(4,128)} %bitcast.16, ...), custom_call_target="tpu_custom_call" | custom-call | tf_op jit(solution)/shard_map/pallas_call | solution.py:545
  44.8 3.1 %shard_map.78 = (f32[896,128]{1,0:T(8,128)}, f32[2048,128]{1,0:T(8,128)}) custom-call(f32[256,1024]{1,0:T(8,128)} %get-tuple-element.8.acc_h, bf16[32,32,128]{2,1,0:T(8,128)(2,1)} %get-tuple-element.9.got_h, s32[8,128]{1,0:T(8,128)} %get-tuple-element.10.code_h, bf16[224,4,128]{2,1,0:T(4,128)(2,1)} %bitcast.15), custom_call_target="tpu_custom_call" | custom-call | tf_op jit(solution)/shard_map/pallas_call | solution.py:606

commit v8 on v7

--- a/solution.py
+++ b/solution.py
@@ -331,9 +331,8 @@
         targets_out(range(4, 8))
         drecv[me] = dsend[me]
 
-        @pl.loop(1, NP)
-        def _(j):
-            dcopy(me ^ j).start()
+        for q in others:
+            dcopy(q).start()
 
     def targets_in():
         many = drecv.at[pl.ds(0, NP - 1)]

time: 48.1 us -> 48.1 us (level)
  no operation moved by 1% of the time
where the time goes in v8:
time: 48.1 us; the launch traced here: 48 us
  Pallas kernels  47.3 us (98%)
  between operations  0.64 us (1%)
    pallas_call x1, Pallas kernels, on_device(): pl.pallas_call(body, out_shape=(jax.ShapeDtypeStruct((256, F * D), F32),...  44.2 us
    pallas_call x1, Pallas kernels, on_device(): pl.pallas_call(finish, out_shape=(jax.ShapeDtypeStruct(((F - 1) * D, D),...  3.16 us

profile of v8, /device:TPU:1, one launch (start us, length us, event | category | flops | bytes accessed | tf_op | source)
XLA Modules:
  0.0 48.0 jit_solution(14129292631092363445)
XLA Ops:
  0.6 44.2 %shard_map.77 = (f32[256,1024]{1,0:T(8,128)}, bf16[32,32,128]{2,1,0:T(8,128)(2,1)}, s32[8,128]{1,0:T(8,128)}, bf16[14,2,8,4,128]{4,3,2,1,0:T(4,128)(2,1)}) custom-call(bf16[1024,128]{1,0:T(8,128)(2,1)} %bitcast.14, bf16[28,128,128]{2,1,0:T(8,128)(2,1)} %bitcast.13, bf16[7,128,128]{2,1,0:T(8,128)(2,1)} %bil_h.1, s32[8,4,128]{2,1,0:T(4,128)} %bitcast.16, ...), custom_call_target="tpu_custom_call" | custom-call | tf_op jit(solution)/shard_map/pallas_call | solution.py:544
  44.8 3.2 %shard_map.78 = (f32[896,128]{1,0:T(8,128)}, f32[2048,128]{1,0:T(8,128)}) custom-call(f32[256,1024]{1,0:T(8,128)} %get-tuple-element.8.acc_h, bf16[32,32,128]{2,1,0:T(8,128)(2,1)} %get-tuple-element.9.got_h, s32[8,128]{1,0:T(8,128)} %get-tuple-element.10.code_h, bf16[224,4,128]{2,1,0:T(4,128)(2,1)} %bitcast.15), custom_call_target="tpu_custom_call" | custom-call | tf_op jit(solution)/shard_map/pallas_call | solution.py:605
